TPU v7x, 32 devices: a whole 2x2x4 slice. The times are simulated.
32 devices in a mesh: px: 4 (over y, x), py: 8 (over z, core).
Axes of the slice: x: 2, y: 2, z: 4, core: 2. Of those that a mesh axis runs over, the one named last changes fastest.
Arguments:
- white_noise: float32 [2, 64, 256, 256], P(None, 'px', 'py'), may hold values from -6 to 6
- spectrum: float32 [64, 256, 256], P('px', 'py'), may hold values from 0.1 to 2, as said below
- group_table: int32 [3, 8], replicated, may hold values from 0 to 7, each once within a row
Outputs:
- modulus: float32 [2, 64, 256, 256], P(None, 'px', 'py')
- level_one: float32 [2, 32, 128, 128], P(None, 'px', 'py')
- level_two: float32 [2, 16, 64, 64], P(None, 'px', 'py')
- level_three: float32 [2, 8, 32, 32], P(None, 'px', 'py')
Inputs may be any that keep to these rules, and one draw needn't show every extreme that they name: spectrum[j, m, k] equals spectrum[(64 - j) % 64, (256 - m) % 256, (256 - k) % 256]. `group_table`: each row is a permutation of 0 to 7.
All inputs are finite; a program needn't handle non-finite values.
Results may differ from a plain program's by a relative error of at most 0.000088.
Values sent between devices are 32-bit elements; how exact they have to be, the bound alone decides.
A program may use at most 192 MiB of HBM per device.

v0:
```python
import math

import jax
import jax.numpy as jnp
from jax import lax
from jax.sharding import PartitionSpec as P


def dft_tables(length, direction):
    positions = lax.iota(jnp.int32, length)
    products = positions[:, None] * positions[None, :] % length
    angles = products.astype(jnp.float32) * (2.0 * math.pi / length)
    return (jnp.cos(angles), direction * jnp.sin(angles))


def complex_apply(stacked, table_cos, table_sin, pattern):
    half_count = stacked.shape[0] // 2
    real_part = stacked[:half_count]
    imag_part = stacked[half_count:]
    real_cos = jnp.einsum(pattern, real_part, table_cos, precision=lax.Precision.HIGHEST)
    imag_sin = jnp.einsum(pattern, imag_part, table_sin, precision=lax.Precision.HIGHEST)
    imag_cos = jnp.einsum(pattern, imag_part, table_cos, precision=lax.Precision.HIGHEST)
    real_sin = jnp.einsum(pattern, real_part, table_sin, precision=lax.Precision.HIGHEST)
    return jnp.concatenate([real_cos - imag_sin, imag_cos + real_sin], 0)


def forward(payload, direction, carried_count):
    leading, length_z, cells_x, cells_y = payload.shape
    size_px = lax.axis_size("px")
    size_py = lax.axis_size("py")
    length_x = size_px * cells_x
    length_y = size_py * cells_y
    kept = leading - carried_count
    y_cos, y_sin = dft_tables(length_y, direction)
    x_cos, x_sin = dft_tables(length_x, direction)
    block_z = length_z // size_py
    blocks = payload.reshape(leading, size_py, block_z, cells_x * cells_y)
    received = lax.all_to_all(blocks, "py", split_axis=1, concat_axis=1, tiled=True)
    received = received.reshape(leading, size_py, block_z, cells_x, cells_y)
    result = complex_apply(
        received,
        y_cos.reshape(size_py, cells_y, length_y),
        y_sin.reshape(size_py, cells_y, length_y),
        "lakxb,abm->lkxm",
    )
    received = lax.all_to_all(result, "px", split_axis=1, concat_axis=2, tiled=True)
    spectral = complex_apply(received, x_cos, x_sin, "lkxm,xj->lkjm")
    return (spectral, received[kept:])


def backward(spectral):
    leading, part_z, length_x, length_y = spectral.shape
    size_px = lax.axis_size("px")
    size_py = lax.axis_size("py")
    cells_x = length_x // size_px
    cells_y = length_y // size_py
    received = lax.all_to_all(spectral, "px", split_axis=2, concat_axis=1, tiled=True)
    block_z = received.shape[1]
    arranged = jnp.transpose(
        received.reshape(leading, block_z, cells_x, size_py, cells_y), (0, 1, 3, 2, 4)
    )
    arranged = arranged.reshape(leading, block_z, size_py, cells_x * cells_y)
    received = lax.all_to_all(arranged, "py", split_axis=2, concat_axis=1, tiled=True)
    return received.reshape(leading, block_z * size_py, cells_x, cells_y)


def coarsen(values):
    members, size_x, size_y, size_z = values.shape
    blocks = values.reshape(members, size_x // 2, 2, size_y // 2, 2, size_z // 2, 2)
    return blocks.mean(axis=(2, 4, 6))


def on_device(white_noise, spectrum, group_table):
    members, cells_x, cells_y, length_z = white_noise.shape
    length_x = cells_x * lax.axis_size("px")
    length_y = cells_y * lax.axis_size("py")
    z_cos, z_sin = dft_tables(length_z, -1.0)
    paired = complex_apply(white_noise, z_cos, z_sin, "fxyz,zk->fkxy")
    spectrum_rows = jnp.transpose(spectrum, (2, 0, 1))[None]
    inverse_cos, inverse_sin = dft_tables(length_z, 1.0)
    spectral, unused = forward(paired, -1.0, 0)
    restored = backward(spectral)
    inverse_z = complex_apply(restored * spectrum_rows, inverse_cos, inverse_sin, "lkxy,kn->lnxy")
    spectral, unused = forward(inverse_z, 1.0, 0)
    restored = backward(spectral)
    fields = jnp.transpose(restored, (0, 2, 3, 1))
    fields = fields * (1.0 / (length_x * length_y * length_z))
    modulus = jnp.exp(0.5 * fields)
    coarse_one = coarsen(modulus)
    coarse_two = coarsen(coarse_one)
    coarse_three = coarsen(coarse_two)
    gathered = (
        lax.all_gather(coarse_one, "py", axis=2, tiled=True),
        lax.all_gather(coarse_two, "py", axis=2, tiled=True),
        lax.all_gather(coarse_three, "py", axis=2, tiled=True),
    )
    column = lax.axis_index("py")
    routed = []
    for level_index in range(3):
        width = gathered[level_index].shape[2] // lax.axis_size("py")
        source_row = group_table[level_index, column]
        routed.append(lax.dynamic_slice_in_dim(gathered[level_index], source_row * width, width, 2))
    return (modulus, routed[0], routed[1], routed[2])


def solution(mesh):
    in_specs = (P(None, "px", "py", None), P("px", "py", None), P())
    out_specs = (
        P(None, "px", "py", None),
        P(None, "px", "py", None),
        P(None, "px", "py", None),
        P(None, "px", "py", None),
    )
    return jax.shard_map(
        on_device, mesh=mesh, in_specs=in_specs, out_specs=out_specs, check_vma=False
    )
```

profile of v0, /device:TPU:0, one launch (start us, length us, event | category | flops | bytes accessed | tf_op | source)
XLA Modules:
  0.0 441.4 jit_solution(7291163717561491544)
XLA Ops:
  7.2 2.7 fusion.16
  9.9 3.4 fusion.12
  13.3 1.6 convolution_subtract_fusion.2
  16.1 2.8 convolution_add_fusion.2
  20.2 1.1 copy.83
  21.2 6.4 %all-to-all-start = ((f32[2,8,32,512]{3,2,0,1:T(8,128)}), f32[2,8,32,512]{3,2,0,1:T(8,128)S(1)}, u32[]{:S(2)}, u32[]{:S(2)}) async-start(f32[2,8,32,512]{3,2,0,1:T(8,128)} %copy.83), calls=%async_computation | async-start | bytes 2097152 | tf_op jit(solution)/shard_map/all_to_all | solution.py:38
  27.8 26.3 %all-to-all-done = f32[2,8,32,512]{3,2,0,1:T(8,128)S(1)} async-done(((f32[2,8,32,512]{3,2,0,1:T(8,128)}), f32[2,8,32,512]{3,2,0,1:T(8,128)S(1)}, u32[]{:S(2)}, u32[]{:S(2)}) %all-to-all-start) | async-done | bytes 1048608 | tf_op jit(solution)/shard_map/all_to_all | solution.py:38
  55.4 1.9 reshape.307
  57.3 2.8 convolution_bitcast_fusion.6
  60.1 2.8 convolution_bitcast_fusion.4
  62.9 2.8 fusion.5
  65.6 3.0 fusion.7
  68.8 17.4 %all_to_all.94 = f32[2,32,16,256]{3,2,0,1:T(8,128)S(1)} all-to-all(f32[2,32,16,256]{3,2,0,1:T(8,128)S(1)} %copy.86), channel_id=1, replica_groups=mesh['px'=4,'py'=8] {'px'}, dimensions={1} | all-to-all | bytes 2097152 | tf_op jit(solution)/shard_map/all_to_all | solution.py:46
  89.9 15.1 %all_to_all.95 = f32[2,8,64,256]{3,1,0,2:T(8,128)S(1)} all-to-all(f32[2,8,64,256]{3,1,0,2:T(8,128)S(1)} %copy.88), channel_id=1, replica_groups=mesh['px'=4,'py'=8] {'px'}, dimensions={2} | all-to-all | bytes 2097152 | tf_op jit(solution)/shard_map/all_to_all | solution.py:57
  105.6 2.5 reshape.311
  108.1 5.0 %copy.120 = f32[2,32,8,16,32]{4,3,1,0,2:T(8,128)} copy(f32[2,32,8,16,32]{4,2,3,1,0:T(8,128)} %bitcast.242) | data formatting | bytes 2097152 | tf_op jit(solution)/shard_map/reshape | solution.py:62
  113.0 3.5 reshape.350
  116.6 30.2 %all_to_all.96 = f32[2,32,8,512]{3,1,0,2:T(8,128)S(1)} all-to-all(f32[2,32,8,512]{3,1,0,2:T(8,128)S(1)} %reshape.350), channel_id=1, replica_groups=mesh['px'=4,'py'=8] {'py'}, dimensions={2} | all-to-all | bytes 2097152 | tf_op jit(solution)/shard_map/all_to_all | solution.py:63
  146.8 2.7 copy.121
  149.4 3.4 reshape.351
  153.1 1.6 fusion.75
  154.7 2.4 fusion.69
  157.1 1.6 fusion.67
  158.6 2.4 fusion.73
  162.3 1.3 add.187
  164.9 29.0 %all_to_all.97 = f32[2,8,32,512]{3,2,0,1:T(8,128)S(1)} all-to-all(f32[2,8,32,512]{3,2,0,1:T(8,128)S(1)} %copy.96), channel_id=1, replica_groups=mesh['px'=4,'py'=8] {'py'}, dimensions={1} | all-to-all | bytes 2097152 | tf_op jit(solution)/shard_map/all_to_all | solution.py:38
  193.9 0.9 fusion.213
  195.7 2.8 convolution_bitcast_fusion.2
  198.7 1.9 reshape.316
  200.6 4.5 %convolution_bitcast_fusion = f32[32,16,256]{2,1,0:T(8,128)S(1)} fusion(f32[8,32,16,32]{3,2,0,1:T(8,128)} %reshape.316, s32[8,32]{1,0:T(8,128)S(1)} %multiply_add_fusion), kind=kOutput, calls=%fused_computation | convolution fusion | flops 403570688 | bytes 1049600 | tf_op jit(solution)/shard_map/lakxb,abm->lkxm/dot_general | solution.py:23
  205.2 2.8 fusion.9
  207.9 3.0 fusion.11
  211.1 16.5 %all_to_all.98 = f32[2,32,16,256]{3,2,0,1:T(8,128)S(1)} all-to-all(f32[2,32,16,256]{3,2,0,1:T(8,128)S(1)} %copy.99), channel_id=1, replica_groups=mesh['px'=4,'py'=8] {'px'}, dimensions={1} | all-to-all | bytes 2097152 | tf_op jit(solution)/shard_map/all_to_all | solution.py:46
  231.3 15.3 %all_to_all.99 = f32[2,8,64,256]{3,1,0,2:T(8,128)S(1)} all-to-all(f32[2,8,64,256]{3,1,0,2:T(8,128)S(1)} %copy.101), channel_id=1, replica_groups=mesh['px'=4,'py'=8] {'px'}, dimensions={2} | all-to-all | bytes 2097152 | tf_op jit(solution)/shard_map/all_to_all | solution.py:57
  247.2 2.5 reshape.320
  249.7 5.0 %copy.124 = f32[2,32,8,16,32]{4,3,1,0,2:T(8,128)} copy(f32[2,32,8,16,32]{4,2,3,1,0:T(8,128)} %bitcast.243) | data formatting | bytes 2097152 | tf_op jit(solution)/shard_map/reshape | solution.py:62
  254.7 3.5 reshape.354
  258.2 30.4 %all_to_all.100 = f32[2,32,8,512]{3,1,0,2:T(8,128)S(1)} all-to-all(f32[2,32,8,512]{3,1,0,2:T(8,128)S(1)} %reshape.354), channel_id=1, replica_groups=mesh['px'=4,'py'=8] {'py'}, dimensions={2} | all-to-all | bytes 2097152 | tf_op jit(solution)/shard_map/all_to_all | solution.py:63
  288.8 2.5 exp.14
  291.4 3.5 copy.108
  294.8 68.4 %reshape.322 = f32[2,8,2,16,2,128,2]{6,5,4,3,2,1,0:T(8,128)} reshape(f32[2,16,32,256]{3,2,1,0:T(8,128)S(1)} %copy.108) | data formatting | bytes 2097152 | tf_op jit(solution)/shard_map/reshape | solution.py:69
  363.2 20.8 %reduce_sum.27 = f32[2,8,16,128]{3,2,1,0:T(8,128)S(1)} reduce(f32[2,8,2,16,2,128,2]{6,5,4,3,2,1,0:T(8,128)} %reshape.322, f32[]{:T(128)} %constant.79.clone.1), dimensions={2,4,6}, to_apply=%region_0.1 | reduce | flops 229376 | bytes 1179652 | tf_op jit(solution)/shard_map/reduce_sum | solution.py:70
  387.3 10.5 %div.24 = f32[2,4,2,8,2,64,2]{6,5,4,3,2,1,0:T(8,128)} reshape(f32[2,8,16,128]{3,2,1,0:T(8,128)} %broadcast_multiply_fusion.1) | data formatting | bytes 262144 | tf_op jit(solution)/shard_map/div | solution.py:70
  397.8 4.1 reduce_sum.28
  401.9 1.1 div.27
  403.1 14.0 %all_gather.11 = f32[2,2,32,32]{3,1,0,2:T(2,128)S(1)} all-gather(f32[2,2,4,32]{3,1,0,2:T(2,128)S(1)} %copy.107), channel_id=1, replica_groups=mesh['px'=4,'py'=8] {'py'}, dimensions={2}, use_global_device_ids=true | all-gather | bytes 18432 | tf_op jit(solution)/shard_map/all_gather | solution.py:95
  417.7 14.2 %all_gather.10 = f32[2,4,64,64]{3,2,1,0:T(8,128)S(1)} all-gather(f32[2,4,8,64]{3,2,1,0:T(8,128)S(1)} %broadcast_multiply_fusion.2), channel_id=1, replica_groups=mesh['px'=4,'py'=8] {'py'}, dimensions={2}, use_global_device_ids=true | all-gather | bytes 147456 | tf_op jit(solution)/shard_map/all_gather | solution.py:94
  432.5 1.6 constant_dynamic-slice_fusion.2
  (72 shorter events, 19.8 us)
Async XLA Ops:
  7.2 6.1 %copy-start.4 = (f32[2,16,32,256]{3,2,1,0:T(8,128)S(1)}, f32[2,16,32,256]{3,2,1,0:T(8,128)}, u32[]{:S(2)}) copy-start(f32[2,16,32,256]{3,2,1,0:T(8,128)} %param.3) | copy-start | bytes 3145732
  21.2 32.9 %all-to-all-start = ((f32[2,8,32,512]{3,2,0,1:T(8,128)}), f32[2,8,32,512]{3,2,0,1:T(8,128)S(1)}, u32[]{:S(2)}, u32[]{:S(2)}) async-start(f32[2,8,32,512]{3,2,0,1:T(8,128)} %copy.83), calls=%async_computation | async-start | bytes 2097152 | tf_op jit(solution)/shard_map/all_to_all | solution.py:38
  27.6 404.9 %all-gather.2.cloned.1.call-start = ((), (), s32[]{:S(2)}) async-start(), calls=%async_computation.8 | async-start | bytes 1179648 | tf_op jit(solution)/shard_map/all_gather | solution.py:93
  57.3 2.8 copy-start
  149.4 3.4 copy-start.5
  195.6 2.8 copy-start.3
  200.6 4.5 %copy-start.1 = (f32[8,32,16,32]{3,2,0,1:T(8,128)S(1)}, f32[8,32,16,32]{3,2,0,1:T(8,128)}, u32[]{:S(2)}) copy-start(f32[8,32,16,32]{3,2,0,1:T(8,128)} %reshape.316) | copy-start | bytes 1572868
  294.8 68.4 %copy-start.2 = (f32[2,16,32,256]{3,2,1,0:T(8,128)}, f32[2,16,32,256]{3,2,1,0:T(8,128)S(1)}, u32[]{:S(2)}) copy-start(f32[2,16,32,256]{3,2,1,0:T(8,128)S(1)} %copy.108) | copy-start | bytes 3145732
  363.2 21.5 %copy-start.6 = (s32[3,8]{1,0:T(4,128)S(1)}, s32[3,8]{1,0:T(4,128)}, u32[]{:S(2)}) copy-start(s32[3,8]{1,0:T(4,128)} %param.5) | copy-start | bytes 292
Sparse Core Ops, SparseCore 0:
  384.8 19.6 all-gather.1
where the time goes:
time: 449 us; the launch traced here: 441 us
  blocking collectives  182 us (41%)
  local copies, waits for them, and re-layouts  133 us (30%)
  matrix products  48.4 us (11%)
  other arithmetic  27.9 us (6%)
  waiting for transfers between devices  26.4 us (6%)
  between operations  17 us (4%)
  starting transfers between devices  6.56 us (1%)
    reshape x1, local copies, waits for them, and re-layouts, coarsen(): values.reshape(members, size_x // 2, 2, size_y // 2, 2, size_z // 2, 2)  68.4 us
    all_to_all x2, blocking collectives, backward(): lax.all_to_all(arranged, 'py', split_axis=2, concat_axis=1, tiled=True)  60.5 us
    all_to_all x2, blocking collectives, forward(): lax.all_to_all(result, 'px', split_axis=1, concat_axis=2, tiled=True)  33.8 us
    all_to_all x2, blocking collectives, backward(): lax.all_to_all(spectral, 'px', split_axis=2, concat_axis=1, tiled=True)  30.3 us
    all_to_all x1, blocking collectives, forward(): lax.all_to_all(blocks, 'py', split_axis=1, concat_axis=1, tiled=True)  29 us
    all_to_all x1, waiting for transfers between devices, forward(): lax.all_to_all(blocks, 'py', split_axis=1, concat_axis=1, tiled=True)  26.3 us
    reduce_sum x3, other arithmetic, coarsen(): return blocks.mean(axis=(2, 4, 6))  25 us
    reshape x4, local copies, waits for them, and re-layouts, backward(): arranged = arranged.reshape(leading, block_z, size_py, cells_x * cells_y)  17 us
  transfers between devices with their start and end apart: 2, of which 1 were waited for; matrix products, arithmetic and copies ran while one was open for 4% of the time, Pallas kernels for 0%

commit v1 on v0

v1 whole, which is shorter than its diff:
```python
import numpy as np

import jax
import jax.numpy as jnp
from jax import lax
from jax.sharding import PartitionSpec as P


def angles_of(length):
    positions = np.arange(length, dtype=np.int64)
    return (positions[:, None] * positions[None, :] % length) * (2.0 * np.pi / length)


def complex_table(length, direction):
    angles = angles_of(length)
    cos, sin = np.cos(angles), direction * np.sin(angles)
    table = np.stack([np.stack([cos, sin], 1), np.stack([-sin, cos], 1)], 0)
    return jnp.asarray(table, jnp.float32)


def half_tables(length):
    angles = angles_of(length)[:, : length // 2]
    ahead = np.stack([np.cos(angles), -np.sin(angles)], 1)
    back = 2.0 * ahead
    nyquist = np.where(np.arange(length) % 2 == 0, 1.0, -1.0)
    ahead[:, 1, 0] = nyquist
    back[:, 0, 0] = 1.0
    back[:, 1, 0] = nyquist
    return jnp.asarray(ahead, jnp.float32), jnp.asarray(back, jnp.float32)


def einsum(pattern, left, right):
    return jnp.einsum(pattern, left, right, precision=lax.Precision.HIGH)


def swap_first(values):
    first = values[:, :, :1]
    turned = jnp.swapaxes(first, 0, 1)
    return jnp.concatenate([turned, values[:, :, 1:]], 2)


def coarsen(values):
    members, size_x, size_y, size_z = values.shape
    blocks = values.reshape(members, size_x // 2, 2, size_y // 2, 2, size_z // 2, 2)
    return blocks.mean(axis=(2, 4, 6))


def on_device(white_noise, spectrum, group_table):
    members, cells_x, cells_y, length_z = white_noise.shape
    size_px, size_py = lax.axis_size("px"), lax.axis_size("py")
    length_x, length_y = cells_x * size_px, cells_y * size_py
    half_z = length_z // 2
    block_py, block = half_z // size_py, half_z // size_py // size_px
    z_ahead, z_back = half_tables(length_z)
    scale = 1.0 / (length_x * length_y * length_z)

    table = jnp.transpose(spectrum, (2, 0, 1))
    last = jnp.broadcast_to(table[half_z : half_z + 1], (size_py, 1, cells_x, cells_y))
    table = jnp.concatenate([table[:half_z].reshape(size_py, block_py, cells_x, cells_y), last], 1)
    table = lax.all_to_all(table, "py", split_axis=0, concat_axis=3, tiled=True)[0]
    last = jnp.broadcast_to(table[block_py:], (size_px, 1, cells_x, length_y))
    table = jnp.concatenate([table[:block_py].reshape(size_px, block, cells_x, length_y), last], 1)
    table = lax.all_to_all(table, "px", split_axis=0, concat_axis=2, tiled=True)[0] * scale
    is_first = (lax.axis_index("px") == 0) & (lax.axis_index("py") == 0)
    other = jnp.where(is_first, table[block:], table[:1])
    tables = jnp.stack([table[:block], jnp.concatenate([other, table[1:block]], 0)], 0)

    values = einsum("fxyz,zck->fckxy", white_noise, z_ahead)
    values = swap_first(values)
    values = lax.all_to_all(values, "py", split_axis=2, concat_axis=4, tiled=True)
    values = einsum("fckxy,cydm->fdkxm", values, complex_table(length_y, -1.0))
    values = lax.all_to_all(values, "px", split_axis=2, concat_axis=3, tiled=True)
    values = einsum("fckxm,cxdj->fdkjm", values, complex_table(length_x, -1.0))
    values = values * tables[:, None]
    values = einsum("fckjm,cjdx->fdkxm", values, complex_table(length_x, 1.0))
    values = lax.all_to_all(values, "px", split_axis=3, concat_axis=2, tiled=True)
    values = einsum("fckxm,cmdy->fdkxy", values, complex_table(length_y, 1.0))
    values = lax.all_to_all(values, "py", split_axis=4, concat_axis=2, tiled=True)
    values = swap_first(values)
    fields = einsum("fckxy,zck->fxyz", values, z_back)
    modulus = jnp.exp(0.5 * fields)

    levels = []
    level = modulus
    for _ in range(3):
        level = coarsen(level)
        levels.append(level)
    pieces = [jnp.reshape(level, (size_py, -1)) for level in levels]
    widths = [piece.shape[1] for piece in pieces]
    joined = jnp.concatenate(pieces, 1)
    spread = lax.all_to_all(joined, "py", split_axis=0, concat_axis=0, tiled=True)
    picked, start = [], 0
    for index, width in enumerate(widths):
        part = spread[:, start : start + width]
        picked.append(jnp.take(part, group_table[index], axis=0))
        start += width
    joined = lax.all_to_all(
        jnp.concatenate(picked, 1), "py", split_axis=0, concat_axis=0, tiled=True
    )
    routed, start = [], 0
    for level, width in zip(levels, widths):
        routed.append(joined[:, start : start + width].reshape(level.shape))
        start += width
    return (modulus, routed[0], routed[1], routed[2])


def solution(mesh):
    in_specs = (P(None, "px", "py", None), P("px", "py", None), P())
    out_specs = (P(None, "px", "py", None),) * 4
    return jax.shard_map(
        on_device, mesh=mesh, in_specs=in_specs, out_specs=out_specs, check_vma=False
    )
```

time: 449 us -> 342 us (0.76)
  blocking collectives: 182 us -> 25.7 us
  matrix products: 48.4 us -> 4.61 us
  waiting for transfers between devices: 26.4 us -> 68.4 us
  local copies, waits for them, and re-layouts: 133 us -> 174 us
  starting transfers between devices: 6.56 us -> 26.8 us
  between operations: 17 us -> 1.64 us
  other arithmetic: 27.9 us -> 34.2 us
    all_to_all x7 -> x2, blocking collectives: 154 us -> 25.7 us  [the longest x1 16.1 us: on_device(): lax.all_to_all(values, 'px', split_axis=3, concat_axis=2, tiled=True)]
    all_to_all x1 -> x6, waiting for transfers between devices: 26.3 us -> 68.4 us  [the longest x1 26.4 us: on_device(): lax.all_to_all(values, 'py', split_axis=4, concat_axis=2, tiled=True)]
    unnamed x16 -> x31, local copies, waits for them, and re-layouts: 4.11 us -> 44.2 us
    dot_general x20 -> x6, matrix products: 40.5 us -> 4.61 us  [einsum(): return jnp.einsum(pattern, left, right, precision=lax.Precision.HIGH)]
    all_gather x2 -> x0, blocking collectives: 28.2 us -> none  [the longest x1 14.2 us: on_device(): lax.all_gather(coarse_two, 'py', axis=2, tiled=True)]
    reshape x8 -> x4, local copies, waits for them, and re-layouts: 28 us -> 2.35 us  [the longest x3 2.04 us: on_device(): routed.append(joined[:, start:start + width].reshape(level.shape))]
    all_to_all x4 -> x8, local copies, waits for them, and re-layouts: 1.39 us -> 25.1 us  [the longest x1 12.9 us: on_device(): lax.all_to_all(values, 'py', split_axis=4, concat_axis=2, tiled=True)]
    all_to_all x1 -> x6, starting transfers between devices: 6.35 us -> 26.8 us  [the longest x1 6.35 us: on_device(): lax.all_to_all(table, 'py', split_axis=0, concat_axis=3, tiled=True)[0]]
  transfers between devices with their start and end apart: 2 -> 6, of which waited for: 1 -> 4; matrix products, arithmetic and copies ran while one was open for 4% -> 10% of each run, Pallas kernels for 0% -> 0%
where the time goes in v1:
time: 342 us; the launch traced here: 336 us
  local copies, waits for them, and re-layouts  174 us (51%)
  waiting for transfers between devices  68.4 us (20%)
  other arithmetic  34.2 us (10%)
  starting transfers between devices  26.8 us (8%)
  blocking collectives  25.7 us (8%)
  matrix products  4.61 us (1%)
    reshape x1, local copies, waits for them, and re-layouts, coarsen(): values.reshape(members, size_x // 2, 2, size_y // 2, 2, size_z // 2, 2)  68.4 us
    unnamed x31, local copies, waits for them, and re-layouts  44.2 us
    all_to_all x1, waiting for transfers between devices, on_device(): lax.all_to_all(values, 'py', split_axis=4, concat_axis=2, tiled=True)  26.4 us
    reduce_sum x3, other arithmetic, coarsen(): return blocks.mean(axis=(2, 4, 6))  25 us
    all_to_all x1, waiting for transfers between devices, on_device(): lax.all_to_all(values, 'py', split_axis=2, concat_axis=4, tiled=True)  22.5 us
    all_to_all x1, blocking collectives, on_device(): lax.all_to_all(values, 'px', split_axis=3, concat_axis=2, tiled=True)  16.1 us
    all_to_all x1, local copies, waits for them, and re-layouts, on_device(): lax.all_to_all(values, 'py', split_axis=4, concat_axis=2, tiled=True)  12.9 us
    all_to_all x1, waiting for transfers between devices, on_device(): lax.all_to_all(values, 'px', split_axis=2, concat_axis=3, tiled=True)  12.5 us
  transfers between devices with their start and end apart: 6, of which 4 were waited for; matrix products, arithmetic and copies ran while one was open for 10% of the time, Pallas kernels for 0%

profile of v1, /device:TPU:0, one launch (start us, length us, event | category | flops | bytes accessed | tf_op | source)
XLA Modules:
  0.0 335.8 jit_solution(13237479351401507157)
XLA Ops:
  0.7 2.4 copy.69
  3.3 1.2 reshape.221
  4.5 6.4 %all-to-all-start.2 = ((f32[8,1,8704]{2,1,0:T(1,128)}), f32[8,1,8704]{2,1,0:T(1,128)S(1)}, u32[]{:S(2)}, u32[]{:S(2)}) async-start(f32[8,1,8704]{2,1,0:T(1,128)} %reshape.221), calls=%async_computation.2 | async-start | bytes 557056 | tf_op jit(solution)/shard_map/all_to_all | solution.py:60
  12.2 4.4 %copy.62 = f32[2,2,128,16,32]{4,3,0,1,2:T(8,128)} copy(f32[2,2,128,16,32]{2,4,3,0,1:T(8,128)S(1)} %pad_maximum_fusion.1) | data formatting | bytes 2097152 | tf_op jit(solution)/shard_map/concatenate | solution.py:39
  16.6 4.8 %reshape.219 = f32[8,1,32768]{2,1,0:T(1,128)} reshape(f32[128,2,2,16,32]{4,3,2,1,0:T(8,128)} %bitcast.161) | data formatting | bytes 2097152
  21.5 5.1 %all-to-all-start = ((f32[8,1,32768]{2,1,0:T(1,128)}), f32[8,1,32768]{2,1,0:T(1,128)S(1)}, u32[]{:S(2)}, u32[]{:S(2)}) async-start(f32[8,1,32768]{2,1,0:T(1,128)} %reshape.219), calls=%async_computation | async-start | bytes 2097152 | tf_op jit(solution)/shard_map/all_to_all | solution.py:70
  27.1 1.3 reduce.1
  28.8 0.6 copy.70
  29.9 0.8 pad_maximum_fusion.3
  30.7 22.5 %all-to-all-done = f32[8,1,32768]{2,1,0:T(1,128)S(1)} async-done(((f32[8,1,32768]{2,1,0:T(1,128)}), f32[8,1,32768]{2,1,0:T(1,128)S(1)}, u32[]{:S(2)}, u32[]{:S(2)}) %all-to-all-start) | async-done | bytes 1048608 | tf_op jit(solution)/shard_map/all_to_all | solution.py:70
  53.1 3.9 %all-to-all-start.3 = ((f32[4,5,16,256]{3,2,1,0:T(8,128)}), f32[4,5,16,256]{3,2,1,0:T(8,128)S(1)}, u32[]{:S(2)}, u32[]{:S(2)}) async-start(f32[4,5,16,256]{3,2,1,0:T(8,128)} %pad_maximum_fusion.3), calls=%async_computation.3 | async-start | bytes 655360 | tf_op jit(solution)/shard_map/all_to_all | solution.py:63
  57.0 3.1 reduce
  60.2 3.3 reshape.220
  63.5 6.6 %copy.64 = f32[2,2,16,16,8,32]{5,4,3,1,2,0:T(8,128)} copy(f32[2,2,16,16,8,32]{5,3,0,1,2,4:T(8,128)} %bitcast.162) | data formatting | bytes 2097152 | tf_op jit(solution)/shard_map/all_to_all | solution.py:70
  70.1 3.4 %reshape.204 = f32[2,2,16,16,256,1]{4,3,1,2,0,5:T(8,128)S(1)} reshape(f32[2,2,16,16,8,32]{5,4,3,1,2,0:T(8,128)} %copy.64) | data formatting | bytes 2097152 | tf_op jit(solution)/shard_map/all_to_all | solution.py:70
  73.6 1.0 convolution_bitcast_fusion.4
  74.6 1.0 copy.65
  75.7 4.3 %all-to-all-start.1 = ((f32[2,2,16,16,256]{4,3,1,0,2:T(8,128)}), f32[2,2,16,16,256]{4,3,1,0,2:T(8,128)S(1)}, u32[]{:S(2)}, u32[]{:S(2)}) async-start(f32[2,2,16,16,256]{4,3,1,0,2:T(8,128)} %copy.65), calls=%async_computation.1 | async-start | bytes 2097152 | tf_op jit(solution)/shard_map/all_to_all | solution.py:72
  80.2 12.5 %all-to-all-done.1 = f32[2,2,16,16,256]{4,3,1,0,2:T(8,128)S(1)} async-done(((f32[2,2,16,16,256]{4,3,1,0,2:T(8,128)}), f32[2,2,16,16,256]{4,3,1,0,2:T(8,128)S(1)}, u32[]{:S(2)}, u32[]{:S(2)}) %all-to-all-start.1) | async-done | bytes 1048608 | tf_op jit(solution)/shard_map/all_to_all | solution.py:72
  92.9 0.6 fusion.1
  93.5 0.6 convolution_bitcast_fusion.2
  94.1 0.8 copy.74
  95.0 16.1 %all_to_all.120 = f32[2,2,4,64,256]{4,1,2,0,3:T(2,128)S(1)} all-to-all(f32[2,2,4,64,256]{4,1,2,0,3:T(2,128)S(1)} %copy.74), channel_id=1, replica_groups=mesh['px'=4,'py'=8] {'px'}, dimensions={3} | all-to-all | bytes 2097152 | tf_op jit(solution)/shard_map/all_to_all | solution.py:76
  111.0 0.6 copy.75
  111.7 1.0 convolution_bitcast_fusion.1
  112.7 8.7 %copy.76 = f32[2,2,16,16,256]{3,1,2,0,4:T(2,128)} copy(f32[2,2,16,16,256]{4,3,1,2,0:T(8,128)S(1)} %convolution_bitcast_fusion.1) | data formatting | bytes 2097152 | tf_op jit(solution)/shard_map/fckxm,cmdy->fdkxy/transpose | solution.py:33
  121.4 13.6 %reshape.223 = f32[8,1,32768]{2,1,0:T(1,128)} reshape(f32[256,2,16,2,16]{4,3,2,1,0:T(2,128)} %bitcast.157) | data formatting | bytes 2097152
  135.0 3.8 %all-to-all-start.5 = ((f32[8,1,32768]{2,1,0:T(1,128)}), f32[8,1,32768]{2,1,0:T(1,128)S(1)}, u32[]{:S(2)}, u32[]{:S(2)}) async-start(f32[8,1,32768]{2,1,0:T(1,128)} %reshape.223), calls=%async_computation.5 | async-start | bytes 2097152 | tf_op jit(solution)/shard_map/all_to_all | solution.py:78
  138.8 26.4 %all-to-all-done.5 = f32[8,1,32768]{2,1,0:T(1,128)S(1)} async-done(((f32[8,1,32768]{2,1,0:T(1,128)}), f32[8,1,32768]{2,1,0:T(1,128)S(1)}, u32[]{:S(2)}, u32[]{:S(2)}) %all-to-all-start.5) | async-done | bytes 1048608 | tf_op jit(solution)/shard_map/all_to_all | solution.py:78
  165.2 3.1 reduce.2
  168.4 14.2 %reshape.224 = f32[256,2,16,2,16]{4,3,2,1,0:T(2,128)} reshape(f32[8,32768]{1,0:T(8,128)S(1)} %reduce.2) | data formatting | bytes 2097152
  182.6 12.9 %copy.77 = f32[2,2,16,16,8,32]{5,3,2,4,1,0:T(8,128)} copy(f32[2,2,16,16,8,32]{3,1,2,0,5,4:T(2,128)} %bitcast.158) | data formatting | bytes 2097152 | tf_op jit(solution)/shard_map/all_to_all | solution.py:78
  195.5 4.4 %slice.116 = f32[2,2,127,16,32]{4,3,2,1,0:T(8,128)} slice(f32[2,2,128,16,32]{4,3,2,1,0:T(8,128)} %bitcast.159), slice={[0:2], [0:2], [1:128], [0:16], [0:32]} | slice | bytes 2080768 | tf_op jit(solution)/shard_map/slice | solution.py:39
  199.9 0.8 slice.115
  200.7 3.8 %copy.104 = f32[2,2,127,16,32]{2,4,1,3,0:T(8,128)S(1)} copy(f32[2,2,127,16,32]{4,3,2,1,0:T(8,128)} %slice.116) | data formatting | bytes 2080768
  205.0 0.7 fusion.3
  205.8 68.4 %reshape.174 = f32[2,8,2,16,2,128,2]{6,5,4,3,2,1,0:T(8,128)} reshape(f32[2,16,32,256]{3,2,1,0:T(8,128)S(1)} %fusion.3) | data formatting | bytes 2097152 | tf_op jit(solution)/shard_map/reshape | solution.py:44
  274.1 20.8 %reduce_sum.27 = f32[2,8,16,128]{3,2,1,0:T(8,128)S(1)} reduce(f32[2,8,2,16,2,128,2]{6,5,4,3,2,1,0:T(8,128)} %reshape.174, f32[]{:T(128)} %constant.71.clone.1), dimensions={2,4,6}, to_apply=%region_0.1 | reduce | flops 229376 | bytes 1179652 | tf_op jit(solution)/shard_map/reduce_sum | solution.py:45
  294.9 9.8 %div.31 = f32[2,4,2,8,2,64,2]{6,5,4,3,2,1,0:T(8,128)} reshape(f32[2,8,16,128]{3,2,1,0:T(8,128)S(1)} %broadcast_multiply_fusion) | data formatting | bytes 262144 | tf_op jit(solution)/shard_map/div | solution.py:45
  304.7 4.1 %reduce_sum.28 = f32[2,4,8,64]{3,2,1,0:T(8,128)S(1)} reduce(f32[2,4,2,8,2,64,2]{6,5,4,3,2,1,0:T(8,128)} %div.31, f32[]{:T(128)} %constant.71.clone.1), dimensions={2,4,6}, to_apply=%region_1.2 | reduce | flops 28672 | bytes 147460 | tf_op jit(solution)/shard_map/reduce_sum | solution.py:45
  308.8 1.1 div.35
  310.3 0.8 all_to_all.106
  311.0 3.4 %all-to-all-start.6 = ((f32[8,1,4672]{2,1,0:T(1,128)}), f32[8,1,4672]{2,1,0:T(1,128)S(1)}, u32[]{:S(2)}, u32[]{:S(2)}) async-start(f32[8,1,4672]{2,1,0:T(1,128)} %all_to_all.106), calls=%async_computation.6 | async-start | bytes 303104 | tf_op jit(solution)/shard_map/all_to_all | solution.py:91
  314.4 6.9 %all-to-all-done.6 = f32[8,1,4672]{2,1,0:T(1,128)S(1)} async-done(((f32[8,1,4672]{2,1,0:T(1,128)}), f32[8,1,4672]{2,1,0:T(1,128)S(1)}, u32[]{:S(2)}, u32[]{:S(2)}) %all-to-all-start.6) | async-done | bytes 149536 | tf_op jit(solution)/shard_map/all_to_all | solution.py:91
  323.6 9.7 %all_to_all.121 = f32[8,1,4672]{2,1,0:T(1,128)S(1)} all-to-all(f32[8,1,4672]{2,1,0:T(1,128)S(1)} %copy.80), channel_id=1, replica_groups=mesh['px'=4,'py'=8] {'py'}, dimensions={0} | all-to-all | bytes 299008 | tf_op jit(solution)/shard_map/all_to_all | solution.py:97
  333.3 0.7 reshape.175
  334.0 0.7 reshape.176
  334.6 0.7 reshape.177
  (76 shorter events, 6.2 us)
Async XLA Ops:
  0.6 10.2 %copy-start = (f32[2,16,32,256]{3,2,1,0:T(8,128)S(1)}, f32[2,16,32,256]{3,2,1,0:T(8,128)}, u32[]{:S(2)}) copy-start(f32[2,16,32,256]{3,2,1,0:T(8,128)} %param.9) | copy-start | bytes 3145732
  0.6 10.2 %copy-start.5 = (f32[256,2,128,1,1]{2,0,4,3,1:T(8,128)S(1)}, f32[256,2,128,1,1]{2,0,4,3,1:T(8,128)}, u32[]{:S(2)}) copy-start(f32[256,2,128,1,1]{2,0,4,3,1:T(8,128)} %constant.80) | copy-start | bytes 786436
  4.5 17.0 %all-to-all-start.2 = ((f32[8,1,8704]{2,1,0:T(1,128)}), f32[8,1,8704]{2,1,0:T(1,128)S(1)}, u32[]{:S(2)}, u32[]{:S(2)}) async-start(f32[8,1,8704]{2,1,0:T(1,128)} %reshape.221), calls=%async_computation.2 | async-start | bytes 557056 | tf_op jit(solution)/shard_map/all_to_all | solution.py:60
  21.5 31.7 %all-to-all-start = ((f32[8,1,32768]{2,1,0:T(1,128)}), f32[8,1,32768]{2,1,0:T(1,128)S(1)}, u32[]{:S(2)}, u32[]{:S(2)}) async-start(f32[8,1,32768]{2,1,0:T(1,128)} %reshape.219), calls=%async_computation | async-start | bytes 2097152 | tf_op jit(solution)/shard_map/all_to_all | solution.py:70
  53.1 22.5 %all-to-all-start.3 = ((f32[4,5,16,256]{3,2,1,0:T(8,128)}), f32[4,5,16,256]{3,2,1,0:T(8,128)S(1)}, u32[]{:S(2)}, u32[]{:S(2)}) async-start(f32[4,5,16,256]{3,2,1,0:T(8,128)} %pad_maximum_fusion.3), calls=%async_computation.3 | async-start | bytes 655360 | tf_op jit(solution)/shard_map/all_to_all | solution.py:63
  70.1 3.4 %copy-start.4 = (f32[2,256,2,256,1,1]{3,1,0,2,5,4:T(8,128)S(1)}, f32[2,256,2,256,1,1]{3,1,0,2,5,4:T(8,128)}, u32[]{:S(2)}) copy-start(f32[2,256,2,256,1,1]{3,1,0,2,5,4:T(8,128)} %constant.81) | copy-start | bytes 3145732
  75.7 17.2 %copy-start.8 = (f32[2,64,2,64,1,1]{1,3,0,2,5,4:T(8,128)S(1)}, f32[2,64,2,64,1,1]{1,3,0,2,5,4:T(8,128)}, u32[]{:S(2)}) copy-start(f32[2,64,2,64,1,1]{1,3,0,2,5,4:T(8,128)} %constant.82) | copy-start | bytes 196612
  75.7 17.1 %all-to-all-start.1 = ((f32[2,2,16,16,256]{4,3,1,0,2:T(8,128)}), f32[2,2,16,16,256]{4,3,1,0,2:T(8,128)S(1)}, u32[]{:S(2)}, u32[]{:S(2)}) async-start(f32[2,2,16,16,256]{4,3,1,0,2:T(8,128)} %copy.65), calls=%async_computation.1 | async-start | bytes 2097152 | tf_op jit(solution)/shard_map/all_to_all | solution.py:72
  80.0 13.5 %copy-start.7 = (f32[2,64,2,64,1,1]{1,3,0,2,5,4:T(8,128)S(1)}, f32[2,64,2,64,1,1]{1,3,0,2,5,4:T(8,128)}, u32[]{:S(2)}) copy-start(f32[2,64,2,64,1,1]{1,3,0,2,5,4:T(8,128)} %constant.83) | copy-start | bytes 196612
  93.5 18.2 %copy-start.3 = (f32[2,256,2,256,1,1]{3,1,0,2,5,4:T(8,128)S(1)}, f32[2,256,2,256,1,1]{3,1,0,2,5,4:T(8,128)}, u32[]{:S(2)}) copy-start(f32[2,256,2,256,1,1]{3,1,0,2,5,4:T(8,128)} %constant.84) | copy-start | bytes 3145732
  121.4 17.3 %copy-start.9 = (s32[3,8]{1,0:T(4,128)S(1)}, s32[3,8]{1,0:T(4,128)}, u32[]{:S(2)}) copy-start(s32[3,8]{1,0:T(4,128)} %param.11) | copy-start | bytes 292
  135.0 30.3 %all-to-all-start.5 = ((f32[8,1,32768]{2,1,0:T(1,128)}), f32[8,1,32768]{2,1,0:T(1,128)S(1)}, u32[]{:S(2)}, u32[]{:S(2)}) async-start(f32[8,1,32768]{2,1,0:T(1,128)} %reshape.223), calls=%async_computation.5 | async-start | bytes 2097152 | tf_op jit(solution)/shard_map/all_to_all | solution.py:78
  199.9 5.1 %copy-start.6 = (f32[256,2,128,1,1]{2,0,1,4,3:T(8,128)S(1)}, f32[256,2,128,1,1]{2,0,1,4,3:T(8,128)}, u32[]{:S(2)}) copy-start(f32[256,2,128,1,1]{2,0,1,4,3:T(8,128)} %constant.85) | copy-start | bytes 786436
  205.7 68.4 %copy-start.2 = (f32[2,16,32,256]{3,2,1,0:T(8,128)}, f32[2,16,32,256]{3,2,1,0:T(8,128)S(1)}, u32[]{:S(2)}) copy-start(f32[2,16,32,256]{3,2,1,0:T(8,128)S(1)} %fusion.3) | copy-start | bytes 3145732
  304.7 30.6 %copy-start.1 = (f32[2,16,32,256]{3,2,1,0:T(8,128)S(1)}, f32[2,16,32,256]{3,2,1,0:T(8,128)}, u32[]{:S(2)}) copy-start(f32[2,16,32,256]{3,2,1,0:T(8,128)} %param.9) | copy-start | bytes 3145732
  311.0 10.3 %all-to-all-start.6 = ((f32[8,1,4672]{2,1,0:T(1,128)}), f32[8,1,4672]{2,1,0:T(1,128)S(1)}, u32[]{:S(2)}, u32[]{:S(2)}) async-start(f32[8,1,4672]{2,1,0:T(1,128)} %all_to_all.106), calls=%async_computation.6 | async-start | bytes 303104 | tf_op jit(solution)/shard_map/all_to_all | solution.py:91

commit v2 on v1

--- a/solution.py
+++ b/solution.py
@@ -3,6 +3,8 @@
 import jax
 import jax.numpy as jnp
 from jax import lax
+from jax.experimental import pallas as pl
+from jax.experimental.pallas import tpu as pltpu
 from jax.sharding import PartitionSpec as P
 
 
@@ -11,11 +13,14 @@
     return (positions[:, None] * positions[None, :] % length) * (2.0 * np.pi / length)
 
 
-def complex_table(length, direction):
+def complex_array(length, direction):
     angles = angles_of(length)
     cos, sin = np.cos(angles), direction * np.sin(angles)
-    table = np.stack([np.stack([cos, sin], 1), np.stack([-sin, cos], 1)], 0)
-    return jnp.asarray(table, jnp.float32)
+    return np.stack([np.stack([cos, sin], 1), np.stack([-sin, cos], 1)], 0)
+
+
+def complex_table(length, direction):
+    return jnp.asarray(complex_array(length, direction), jnp.float32)
 
 
 def half_tables(length):
@@ -45,7 +50,7 @@
     return blocks.mean(axis=(2, 4, 6))
 
 
-def on_device(white_noise, spectrum, group_table):
+def general_path(white_noise, spectrum, group_table):
     members, cells_x, cells_y, length_z = white_noise.shape
     size_px, size_py = lax.axis_size("px"), lax.axis_size("py")
     length_x, length_y = cells_x * size_px, cells_y * size_py
@@ -104,6 +109,344 @@
     return (modulus, routed[0], routed[1], routed[2])
 
 
+LANES = 128
+
+
+def dot(left, right):
+    return jnp.dot(
+        left, right, precision=lax.Precision.HIGHEST, preferred_element_type=jnp.float32
+    )
+
+
+def lane_of(shape):
+    return lax.broadcasted_iota(jnp.int32, shape, len(shape) - 1)
+
+
+def exchange(arrays, width):
+    arrays = list(arrays)
+    lane = lane_of(arrays[0].shape)
+    distance = 1
+    while distance < len(arrays):
+        step = distance * width
+        low = (lane // step) % 2 == 0
+        for index in range(len(arrays)):
+            if (index // distance) % 2 == 0:
+                first, second = arrays[index], arrays[index + distance]
+                arrays[index] = jnp.where(low, first, pltpu.roll(second, step, 1))
+                arrays[index + distance] = jnp.where(
+                    low, pltpu.roll(first, LANES - step, 1), second
+                )
+        distance *= 2
+    return arrays
+
+
+def swap_slot(first, second):
+    at_zero = lane_of(first.shape) == 0
+    return jnp.where(at_zero, second, first), jnp.where(at_zero, first, second)
+
+
+def z_forward_kernel(sizes, noise_ref, spectrum_ref, table_ref, out_ref, held):
+    lo, hi, kept = sizes
+    cells_y = noise_ref.shape[2]
+    for f in range(2):
+        rows = noise_ref[f].reshape(lo * hi * cells_y, noise_ref.shape[3])
+        held[f] = dot(rows, table_ref[...])
+
+    def tile(f, c, x):
+        return held[f, pl.ds(x * cells_y, cells_y), pl.ds(c * LANES, LANES)]
+
+    for xh in range(hi):
+        tiles = {}
+        for xl in range(lo):
+            x = xh * lo + xl
+            mixed = swap_slot(tile(0, 1, x), tile(1, 0, x))
+            members = ((tile(0, 0, x), mixed[0]), (mixed[1], tile(1, 1, x)))
+            for f in range(2):
+                for c in range(2):
+                    tiles[f, c, xl] = members[f][c]
+        for f in range(2):
+            for c in range(2):
+                moved = exchange([tiles[f, c, xl] for xl in range(lo)], kept)
+                for p in range(lo):
+                    out_ref[p, (f * 2 + c) * hi + xh] = moved[p]
+    group = lane_of((cells_y, LANES))
+    last = jnp.zeros((cells_y, LANES), jnp.float32)
+    for xh in range(hi):
+        names = [xh * lo + xl for xl in range(lo)]
+        moved = exchange([spectrum_ref[x, :, pl.ds(0, LANES)] for x in names], kept)
+        for p in range(lo):
+            out_ref[p, 4 * hi + xh] = moved[p]
+        for xl in range(lo):
+            value = spectrum_ref[names[xl], :, pl.ds(LANES, 1)]
+            last = jnp.where(group == xl * kept + xh, value, last)
+    for p in range(lo):
+        out_ref[p, 5 * hi] = last
+
+
+def y_forward_kernel(sizes, in_ref, table_ref, out_ref):
+    lo, hi, kept = sizes
+    length_y = table_ref.shape[1]
+    ranks = 2 * hi
+    half = length_y // 2
+
+    def whole(t):
+        return in_ref[:, t].reshape(length_y, LANES)
+
+    for f in range(2):
+        arrays = [None] * ranks
+        for xh in range(hi):
+            pair = [whole((f * 2 + c) * hi + xh) for c in range(2)]
+            product = dot(table_ref[...], jnp.concatenate(pair, 1))
+            by_cos, by_sin = product[:length_y], product[length_y:]
+            arrays[xh] = by_cos[:, :LANES] + by_sin[:, LANES:]
+            arrays[hi + xh] = by_cos[:, LANES:] - by_sin[:, :LANES]
+        moved = exchange(arrays, kept // ranks)
+        for r in range(ranks):
+            out_ref[r, pl.ds(f * length_y, length_y)] = moved[r]
+    halves = []
+    for mh in range(2):
+        for xh in range(hi):
+            halves.append(whole(4 * hi + xh)[mh * half : (mh + 1) * half])
+    moved = exchange(halves, kept // ranks)
+    last = whole(5 * hi)
+    packed = last[:half] + pltpu.roll(last[half:], hi, 1)
+    for r in range(ranks):
+        out_ref[r, pl.ds(2 * length_y, half)] = moved[r]
+        out_ref[r, pl.ds(2 * length_y + half, half)] = packed
+
+
+def x_kernel(sizes, first_ref, in_ref, ahead_ref, back_ref, out_ref):
+    lo, hi, kept = sizes
+    ranks = 2 * hi
+    length_y = out_ref.shape[1] // 2
+    half = length_y // 2
+    lane = lane_of((half, LANES))
+    low = (lane // (hi * ranks)) % 2 == 0
+    parts = [in_ref[r, pl.ds(2 * length_y, half)] for r in range(ranks)]
+    tables = []
+    for part in exchange(parts, 1):
+        upper = jnp.where(low, part, pltpu.roll(part, hi * ranks, 1))
+        lower = jnp.where(low, pltpu.roll(part, LANES - hi * ranks, 1), part)
+        tables.append(jnp.concatenate([upper, lower], 0))
+    last = [in_ref[r, pl.ds(2 * length_y + half, half)] for r in range(ranks)]
+    last = jnp.concatenate(last, 1)
+    source = lax.broadcasted_iota(jnp.int32, (ranks * LANES, LANES), 0)
+    target = lax.broadcasted_iota(jnp.int32, (ranks * LANES, LANES), 1)
+    same = (source // LANES == target % ranks) & ((source % LANES) // kept == target // kept)
+    level = (target // ranks) % hi
+    picked = []
+    for mh in range(2):
+        chosen = same & (source % kept == mh * hi + level)
+        picked.append(dot(last, chosen.astype(jnp.float32)))
+    last = jnp.concatenate(picked, 0)
+    is_first = lax.broadcasted_iota(jnp.int32, last.shape, 0) * 0 + first_ref[0] == 1
+    other = jnp.where(is_first, last, tables[0])
+    for f in range(2):
+        rows = pl.ds(f * length_y, length_y)
+        arrays = exchange([in_ref[r, rows] for r in range(ranks)], 1)
+        for q in range(ranks):
+            table = other if f == 1 and q == 0 else tables[q]
+            arrays[q] = dot(dot(arrays[q], ahead_ref[...]) * table, back_ref[...])
+        arrays = exchange(arrays, 1)
+        for r in range(ranks):
+            out_ref[r, rows] = arrays[r]
+
+
+def y_back_kernel(sizes, in_ref, table_ref, out_ref):
+    lo, hi, kept = sizes
+    ranks = 2 * hi
+    length_y = table_ref.shape[1]
+    cells_y = length_y // lo
+    for f in range(2):
+        rows = pl.ds(f * length_y, length_y)
+        arrays = exchange([in_ref[r, rows] for r in range(ranks)], kept // ranks)
+        for xh in range(hi):
+            product = dot(table_ref[...], jnp.concatenate([arrays[xh], arrays[hi + xh]], 1))
+            by_cos, by_sin = product[:length_y], product[length_y:]
+            real = by_cos[:, :LANES] - by_sin[:, LANES:]
+            imag = by_cos[:, LANES:] + by_sin[:, :LANES]
+            out_ref[:, (f * 2) * hi + xh] = real.reshape(lo, cells_y, LANES)
+            out_ref[:, (f * 2 + 1) * hi + xh] = imag.reshape(lo, cells_y, LANES)
+
+
+def pool_matrix(rows, columns, weight, transposed):
+    long_axis = 0 if transposed else 1
+    shape = (columns, rows) if transposed else (rows, columns)
+    long = lax.broadcasted_iota(jnp.int32, shape, long_axis)
+    short = lax.broadcasted_iota(jnp.int32, shape, 1 - long_axis)
+    return jnp.where(long // 2 == short, weight, 0.0).astype(jnp.float32)
+
+
+def pool_rows(cells_x, cells_y):
+    shape = (cells_x * cells_y // 4, cells_x * cells_y)
+    short = lax.broadcasted_iota(jnp.int32, shape, 0)
+    long = lax.broadcasted_iota(jnp.int32, shape, 1)
+    same_x = long // (2 * cells_y) == short // (cells_y // 2)
+    same_y = (long % cells_y) // 2 == short % (cells_y // 2)
+    return jnp.where(same_x & same_y, 0.125, 0.0).astype(jnp.float32)
+
+
+def z_back_kernel(sizes, in_ref, table_ref, modulus_ref, coarse_ref, held):
+    lo, hi, kept = sizes
+    cells_y = in_ref.shape[2]
+    cells_x = lo * hi
+    length_z = table_ref.shape[0]
+    for xh in range(hi):
+        tiles = {}
+        for f in range(2):
+            for c in range(2):
+                arrays = [in_ref[p, (f * 2 + c) * hi + xh] for p in range(lo)]
+                tiles[f, c] = exchange(arrays, kept)
+        for xl in range(lo):
+            mixed = swap_slot(tiles[0, 1][xl], tiles[1, 0][xl])
+            members = ((tiles[0, 0][xl], mixed[0]), (mixed[1], tiles[1, 1][xl]))
+            rows = pl.ds((xh * lo + xl) * cells_y, cells_y)
+            for f in range(2):
+                for c in range(2):
+                    held[f, rows, pl.ds(c * LANES, LANES)] = members[f][c]
+    coarse_ref[...] = jnp.zeros(coarse_ref.shape, jnp.float32)
+    for f in range(2):
+        values = jnp.exp(0.5 * dot(held[f], table_ref[...]))
+        modulus_ref[f] = values.reshape(cells_x, cells_y, length_z)
+        size_x, size_y, size_z = cells_x, cells_y, length_z
+        start = 0
+        for _ in range(3):
+            right = pool_matrix(size_z // 2, size_z, 1.0, True)
+            values = dot(pool_rows(size_x, size_y), dot(values, right))
+            size_x, size_y, size_z = size_x // 2, size_y // 2, size_z // 2
+            height = 2 * size_x * size_y // lo
+            for d in range(lo // 2):
+                piece = values[d * height : (d + 1) * height]
+                place = (f * lo // 2 + d, pl.ds(start, height), pl.ds(0, size_z))
+                coarse_ref[place] = piece
+            start += height
+
+
+def pick_kernel(heights, table_ref, in_ref, out_ref):
+    for column in range(in_ref.shape[0]):
+        start = 0
+        for index, height in enumerate(heights):
+            rows = pl.ds(start, height)
+            out_ref[column, rows] = in_ref[table_ref[index, column], rows]
+            start += height
+
+
+def lanes_path(white_noise, spectrum, group_table):
+    members, cells_x, cells_y, length_z = white_noise.shape
+    size_px, size_py = lax.axis_size("px"), lax.axis_size("py")
+    length_x, length_y = cells_x * size_px, cells_y * size_py
+    lo, hi = size_py, cells_x // size_py
+    kept = LANES // size_py
+    sizes = (lo, hi, kept)
+    f32 = jnp.float32
+    params = pltpu.CompilerParams(vmem_limit_bytes=48 * 1024 * 1024)
+
+    def call(body, shapes, *operands, scratch=(), scalars=0):
+        out = [jax.ShapeDtypeStruct(shape, f32) for shape in shapes]
+        specs = [pl.BlockSpec(memory_space=pltpu.SMEM)] * scalars
+        specs += [pl.BlockSpec(memory_space=pltpu.VMEM)] * (len(operands) - scalars)
+        return pl.pallas_call(
+            body,
+            out_shape=out,
+            in_specs=specs,
+            out_specs=[pl.BlockSpec(memory_space=pltpu.VMEM)] * len(out),
+            scratch_shapes=list(scratch),
+            compiler_params=params,
+        )(*operands)
+
+    def spread(values, axis):
+        return lax.all_to_all(values, axis, split_axis=0, concat_axis=0, tiled=True)
+
+    z_ahead, z_back = half_tables(length_z)
+    z_ahead = z_ahead.reshape(length_z, length_z)
+    z_back = z_back.reshape(length_z, length_z).T * (1.0 / (length_x * length_y * length_z))
+    angles = angles_of(length_y)
+    y_table = jnp.asarray(np.concatenate([np.cos(angles), np.sin(angles)], 0), f32)
+    lane = np.arange(LANES)
+    part = (lane // (hi * size_px)) % 2
+    place = (lane % size_px) * cells_x + (lane // size_px % hi) * lo + lane // kept
+
+    def x_table(direction):
+        table = complex_array(length_x, direction)
+        rows = table[part, place]
+        return jnp.asarray(rows[:, part, place], f32)
+
+    first = (lax.axis_index("px") == 0) & (lax.axis_index("py") == 0)
+    first = first.astype(jnp.int32).reshape(1)
+    held = pltpu.VMEM((members, cells_x * cells_y, length_z), f32)
+
+    def bind(body):
+        def bound(*refs):
+            body(sizes, *refs)
+
+        return bound
+
+    tiles = 4 * hi
+    (values,) = call(
+        bind(z_forward_kernel),
+        [(size_py, tiles + hi + 1, cells_y, LANES)],
+        white_noise,
+        spectrum,
+        z_ahead,
+        scratch=[held],
+    )
+    values = spread(values, "py")
+    (values,) = call(
+        bind(y_forward_kernel), [(size_px, 3 * length_y, LANES)], values, y_table
+    )
+    values = spread(values, "px")
+    (values,) = call(
+        bind(x_kernel),
+        [(size_px, 2 * length_y, LANES)],
+        first,
+        values,
+        x_table(-1.0),
+        x_table(1.0),
+        scalars=1,
+    )
+    values = spread(values, "px")
+    (values,) = call(
+        bind(y_back_kernel), [(size_py, tiles, cells_y, LANES)], values, y_table
+    )
+    values = spread(values, "py")
+    shapes = []
+    heights = []
+    size = (cells_x, cells_y, length_z)
+    for _ in range(3):
+        size = tuple(extent // 2 for extent in size)
+        shapes.append((members,) + size)
+        heights.append(members * size[0] * size[1] // size_py)
+    modulus, coarse = call(
+        bind(z_back_kernel),
+        [white_noise.shape, (size_py, sum(heights), LANES)],
+        values,
+        z_back,
+        scratch=[held],
+    )
+    coarse = spread(coarse, "py")
+
+    def pick(*refs):
+        pick_kernel(heights, *refs)
+
+    (coarse,) = call(pick, [coarse.shape], group_table, coarse, scalars=1)
+    coarse = spread(coarse, "py")
+    routed, start = [], 0
+    for shape, height in zip(shapes, heights):
+        routed.append(coarse[:, start : start + height, : shape[3]].reshape(shape))
+        start += height
+    return (modulus, routed[0], routed[1], routed[2])
+
+
+def on_device(white_noise, spectrum, group_table):
+    members, cells_x, cells_y, length_z = white_noise.shape
+    size_px, size_py = lax.axis_size("px"), lax.axis_size("py")
+    fits = members == 2 and length_z == 2 * LANES and 2 * cells_x * size_px == LANES
+    fits = fits and cells_x * 2 == size_px * size_py
+    fits = fits and size_px * size_px * size_py == LANES
+    chosen = lanes_path if fits else general_path
+    return chosen(white_noise, spectrum, group_table)
+
+
 def solution(mesh):
     in_specs = (P(None, "px", "py", None), P("px", "py", None), P())
     out_specs = (P(None, "px", "py", None),) * 4

time: 342 us -> 154 us (0.45); the launches traced: 336 us -> 154 us
  local copies, waits for them, and re-layouts: 174 us -> 5.12 us
  blocking collectives: 25.7 us -> 108 us
  waiting for transfers between devices: 68.4 us -> 19.2 us
  other arithmetic: 34.2 us -> 0 us
  starting transfers between devices: 26.8 us -> 3.85 us
  Pallas kernels: 0 us -> 16.6 us
  matrix products: 4.61 us -> 0 us
    all_to_all x2 -> x5, blocking collectives: 25.7 us -> 108 us  [spread(): return lax.all_to_all(values, axis, split_axis=0, concat_axis=0, tiled=True)]
    reshape x5 -> x0, local copies, waits for them, and re-layouts: 70.7 us -> none  [the longest x1 68.4 us: coarsen(): values.reshape(members, size_x // 2, 2, size_y // 2, 2, size_z // 2, 2)]
    all_to_all x6 -> x1, waiting for transfers between devices: 68.4 us -> 19.2 us  [spread(): return lax.all_to_all(values, axis, split_axis=0, concat_axis=0, tiled=True)]
    unnamed x31 -> x16, local copies, waits for them, and re-layouts: 44.2 us -> 3.24 us
    all_to_all x8 -> x0, local copies, waits for them, and re-layouts: 25.1 us -> none  [the longest x1 12.9 us: on_device(): lax.all_to_all(values, 'py', split_axis=4, concat_axis=2, tiled=True)]
    reduce_sum x3 -> x0, other arithmetic: 25 us -> none  [coarsen(): return blocks.mean(axis=(2, 4, 6))]
    all_to_all x6 -> x1, starting transfers between devices: 26.8 us -> 3.85 us  [spread(): return lax.all_to_all(values, axis, split_axis=0, concat_axis=0, tiled=True)]
    pallas_call x0 -> x6, Pallas kernels: none -> 16.6 us  [call(): pl.pallas_call(body, out_shape=out, in_specs=specs, out_specs=[pl.BlockSp...]
  transfers between devices with their start and end apart: 6 -> 1, of which waited for: 4 -> 1; matrix products, arithmetic and copies ran while one was open for 10% -> 0% of each run, Pallas kernels for 0% -> 0%
where the time goes in v2:
time: 154 us
  blocking collectives  108 us (70%)
  waiting for transfers between devices  19.2 us (12%)
  Pallas kernels  16.6 us (11%)
  local copies, waits for them, and re-layouts  5.12 us (3%)
  starting transfers between devices  3.85 us (2%)
    all_to_all x5, blocking collectives, spread(): return lax.all_to_all(values, axis, split_axis=0, concat_axis=0, tiled=True)  108 us
    all_to_all x1, waiting for transfers between devices, spread(): return lax.all_to_all(values, axis, split_axis=0, concat_axis=0, tiled=True)  19.2 us
    pallas_call x6, Pallas kernels, call(): pl.pallas_call(body, out_shape=out, in_specs=specs, out_specs=[pl.BlockSp...  16.6 us
    all_to_all x1, starting transfers between devices, spread(): return lax.all_to_all(values, axis, split_axis=0, concat_axis=0, tiled=True)  3.85 us
    unnamed x16, local copies, waits for them, and re-layouts  3.24 us
  transfers between devices with their start and end apart: 1, of which 1 were waited for; matrix products, arithmetic and copies ran while one was open for 0% of the time, Pallas kernels for 0%

profile of v2, /device:TPU:0, one launch (start us, length us, event | category | flops | bytes accessed | tf_op | source)
XLA Modules:
  0.0 153.6 jit_solution(4903610042973827512)
XLA Ops:
  0.6 0.0 copy-start.1
  0.6 1.2 copy-done.1
  1.9 0.0 copy-start.2
  1.9 1.0 copy-done.2
  2.9 0.0 copy-start.4
  2.9 0.9 copy-done.4
  3.8 1.8 %shard_map.111 = f32[8,11,32,128]{3,2,1,0:T(8,128)S(1)} custom-call(f32[2,16,32,256]{3,2,1,0:T(8,128)S(1)} %copy-done.1, f32[16,32,256]{2,1,0:T(8,128)S(1)} %copy-done.2, f32[256,256]{1,0:T(8,128)S(1)} %copy-done.4), custom_call_target="tpu_custom_call" | custom-call | tf_op jit(solution)/shard_map/pallas_call | solution.py:348
  5.6 0.0 copy-start
  5.7 41.3 %all_to_all.30.refs_0_ = f32[8,11,32,128]{3,2,1,0:T(8,128)S(1)} all-to-all(f32[8,11,32,128]{3,2,1,0:T(8,128)S(1)} %shard_map.111), channel_id=1, replica_groups=mesh['px'=4,'py'=8] {'py'}, dimensions={0} | all-to-all | bytes 2883584 | tf_op jit(solution)/shard_map/all_to_all | solution.py:358
  46.9 0.0 copy-done
  46.9 3.3 %shard_map.112 = f32[4,768,128]{2,1,0:T(8,128)} custom-call(f32[8,11,32,128]{3,2,1,0:T(8,128)S(1)} %all_to_all.30.refs_0_, f32[512,256]{1,0:T(8,128)S(1)} %copy-done), custom_call_target="tpu_custom_call" | custom-call | tf_op jit(solution)/shard_map/pallas_call | solution.py:348
  50.2 0.0 copy-start.5
  50.2 0.0 copy-start.6
  50.2 3.8 %all-to-all-start.1 = ((f32[4,768,128]{2,1,0:T(8,128)}), f32[4,768,128]{2,1,0:T(8,128)S(1)}, u32[]{:S(2)}, u32[]{:S(2)}) async-start(f32[4,768,128]{2,1,0:T(8,128)} %shard_map.112), calls=%async_computation.1 | async-start | bytes 3145728 | tf_op jit(solution)/shard_map/all_to_all | solution.py:358
  54.1 19.2 %all-to-all-done.1.refs_1_ = f32[4,768,128]{2,1,0:T(8,128)S(1)} async-done(((f32[4,768,128]{2,1,0:T(8,128)}), f32[4,768,128]{2,1,0:T(8,128)S(1)}, u32[]{:S(2)}, u32[]{:S(2)}) %all-to-all-start.1) | async-done | bytes 1572896 | tf_op jit(solution)/shard_map/all_to_all | solution.py:358
  73.2 0.0 copy-done.5
  73.3 0.0 copy-done.6
  73.3 2.8 %shard_map.113 = f32[4,512,128]{2,1,0:T(8,128)S(1)} custom-call(s32[1]{0:T(128)} %bitcast.refs_0_, f32[4,768,128]{2,1,0:T(8,128)S(1)} %all-to-all-done.1.refs_1_, f32[128,128]{1,0:T(8,128)S(1)} %copy-done.6, f32[128,128]{1,0:T(8,128)S(1)} %copy-done.5), custom_call_target="tpu_custom_call" | custom-call | tf_op jit(solution)/shard_map/pallas_call | solution.py:348
  76.1 16.1 %all_to_all.31.refs_0_ = f32[4,512,128]{2,1,0:T(8,128)S(1)} all-to-all(f32[4,512,128]{2,1,0:T(8,128)S(1)} %shard_map.113), channel_id=1, replica_groups=mesh['px'=4,'py'=8] {'px'}, dimensions={0} | all-to-all | bytes 2097152 | tf_op jit(solution)/shard_map/all_to_all | solution.py:358
  92.1 2.1 %shard_map.114 = f32[8,8,32,128]{3,2,1,0:T(8,128)S(1)} custom-call(f32[4,512,128]{2,1,0:T(8,128)S(1)} %all_to_all.31.refs_0_, f32[512,256]{1,0:T(8,128)S(1)} %copy-done), custom_call_target="tpu_custom_call" | custom-call | tf_op jit(solution)/shard_map/pallas_call | solution.py:348
  94.3 0.0 copy-start.3
  94.3 0.0 copy-start.7
  94.3 29.5 %all_to_all.32.refs_0_ = f32[8,8,32,128]{3,2,1,0:T(8,128)S(1)} all-to-all(f32[8,8,32,128]{3,2,1,0:T(8,128)S(1)} %shard_map.114), channel_id=1, replica_groups=mesh['px'=4,'py'=8] {'py'}, dimensions={0} | all-to-all | bytes 2097152 | tf_op jit(solution)/shard_map/all_to_all | solution.py:358
  123.8 0.0 copy-done.3
  123.8 5.9 %shard_map.115 = (f32[2,16,32,256]{3,2,1,0:T(8,128)}, f32[8,42,128]{2,1,0:T(8,128)S(1)}) custom-call(f32[8,8,32,128]{3,2,1,0:T(8,128)S(1)} %all_to_all.32.refs_0_, f32[256,256]{1,0:T(8,128)S(1)} %copy-done.3), custom_call_target="tpu_custom_call" | custom-call | tf_op jit(solution)/shard_map/pallas_call | solution.py:348
  129.7 10.7 %all_to_all.33.refs_1_ = f32[8,42,128]{2,1,0:T(8,128)S(1)} all-to-all(f32[8,42,128]{2,1,0:T(8,128)S(1)} %get-tuple-element.7), channel_id=1, replica_groups=mesh['px'=4,'py'=8] {'py'}, dimensions={0} | all-to-all | bytes 344064 | tf_op jit(solution)/shard_map/all_to_all | solution.py:358
  140.4 0.0 copy-done.7
  140.4 0.6 shard_map.116
  141.0 10.7 %all_to_all.34 = f32[8,42,128]{2,1,0:T(8,128)S(1)} all-to-all(f32[8,42,128]{2,1,0:T(8,128)S(1)} %shard_map.116), channel_id=1, replica_groups=mesh['px'=4,'py'=8] {'py'}, dimensions={0} | all-to-all | bytes 344064 | tf_op jit(solution)/shard_map/all_to_all | solution.py:358
  151.7 0.6 slice.14
  152.3 0.6 slice.13
  153.0 0.7 slice.12
Async XLA Ops:
  0.6 1.2 copy-start.1
  1.9 1.0 copy-start.2
  2.9 0.9 copy-start.4
  5.6 41.3 %copy-start = (f32[512,256]{1,0:T(8,128)S(1)}, f32[512,256]{1,0:T(8,128)}, u32[]{:S(2)}) copy-start(f32[512,256]{1,0:T(8,128)} %constant.24.clone.refs_1_) | copy-start | bytes 1572868
  50.2 23.0 %copy-start.5 = (f32[128,128]{1,0:T(8,128)S(1)}, f32[128,128]{1,0:T(8,128)}, u32[]{:S(2)}) copy-start(f32[128,128]{1,0:T(8,128)} %constant.26.clone.refs_3_) | copy-start | bytes 196612
  50.2 23.0 %copy-start.6 = (f32[128,128]{1,0:T(8,128)S(1)}, f32[128,128]{1,0:T(8,128)}, u32[]{:S(2)}) copy-start(f32[128,128]{1,0:T(8,128)} %constant.25.clone.refs_2_) | copy-start | bytes 196612
  50.2 23.0 %all-to-all-start.1 = ((f32[4,768,128]{2,1,0:T(8,128)}), f32[4,768,128]{2,1,0:T(8,128)S(1)}, u32[]{:S(2)}, u32[]{:S(2)}) async-start(f32[4,768,128]{2,1,0:T(8,128)} %shard_map.112), calls=%async_computation.1 | async-start | bytes 3145728 | tf_op jit(solution)/shard_map/all_to_all | solution.py:358
  94.3 29.5 %copy-start.3 = (f32[256,256]{1,0:T(8,128)S(1)}, f32[256,256]{1,0:T(8,128)}, u32[]{:S(2)}) copy-start(f32[256,256]{1,0:T(8,128)} %constant.30.refs_1_) | copy-start | bytes 786436
  94.3 46.1 %copy-start.7 = (s32[3,8]{1,0:T(4,128)S(1)}, s32[3,8]{1,0:T(4,128)}, u32[]{:S(2)}) copy-start(s32[3,8]{1,0:T(4,128)} %refs_0_.3) | copy-start | bytes 292

commit v3 on v2

--- a/solution.py
+++ b/solution.py
@@ -110,6 +110,7 @@
 
 
 LANES = 128
+MESH = pl.DeviceIdType.MESH
 
 
 def dot(left, right):
@@ -331,6 +332,54 @@
             start += height
 
 
+def spread_kernel(axis, in_ref, out_ref, own_sem, send_sems, recv_sems):
+    count = in_ref.shape[0]
+    me = lax.axis_index(axis)
+    barrier = pltpu.get_barrier_semaphore()
+    for away in range(1, count):
+        peer = lax.rem(me + away, count)
+        pl.semaphore_signal(barrier, inc=1, device_id={axis: peer}, device_id_type=MESH)
+    own = pltpu.make_async_copy(in_ref.at[me], out_ref.at[me], own_sem)
+    own.start()
+    pl.semaphore_wait(barrier, count - 1)
+    copies = []
+    for away in range(1, count):
+        peer = lax.rem(me + away, count)
+        copy = pltpu.make_async_remote_copy(
+            src_ref=in_ref.at[peer],
+            dst_ref=out_ref.at[me],
+            send_sem=send_sems.at[away],
+            recv_sem=recv_sems.at[away],
+            device_id={axis: peer},
+            device_id_type=MESH,
+        )
+        copy.start()
+        copies.append(copy)
+    own.wait()
+    for copy in copies:
+        copy.wait()
+
+
+def spread_call(values, axis, number):
+    count = values.shape[0]
+
+    def body(*refs):
+        spread_kernel(axis, *refs)
+
+    return pl.pallas_call(
+        body,
+        out_shape=jax.ShapeDtypeStruct(values.shape, values.dtype),
+        in_specs=[pl.BlockSpec(memory_space=pltpu.VMEM)],
+        out_specs=pl.BlockSpec(memory_space=pltpu.VMEM),
+        scratch_shapes=[
+            pltpu.SemaphoreType.DMA,
+            pltpu.SemaphoreType.DMA((count,)),
+            pltpu.SemaphoreType.DMA((count,)),
+        ],
+        compiler_params=pltpu.CompilerParams(collective_id=number, has_side_effects=True),
+    )(values)
+
+
 def lanes_path(white_noise, spectrum, group_table):
     members, cells_x, cells_y, length_z = white_noise.shape
     size_px, size_py = lax.axis_size("px"), lax.axis_size("py")
@@ -354,9 +403,6 @@
             compiler_params=params,
         )(*operands)
 
-    def spread(values, axis):
-        return lax.all_to_all(values, axis, split_axis=0, concat_axis=0, tiled=True)
-
     z_ahead, z_back = half_tables(length_z)
     z_ahead = z_ahead.reshape(length_z, length_z)
     z_back = z_back.reshape(length_z, length_z).T * (1.0 / (length_x * length_y * length_z))
@@ -390,11 +436,11 @@
         z_ahead,
         scratch=[held],
     )
-    values = spread(values, "py")
+    values = spread_call(values, "py", 0)
     (values,) = call(
         bind(y_forward_kernel), [(size_px, 3 * length_y, LANES)], values, y_table
     )
-    values = spread(values, "px")
+    values = spread_call(values, "px", 1)
     (values,) = call(
         bind(x_kernel),
         [(size_px, 2 * length_y, LANES)],
@@ -404,11 +450,11 @@
         x_table(1.0),
         scalars=1,
     )
-    values = spread(values, "px")
+    values = spread_call(values, "px", 2)
     (values,) = call(
         bind(y_back_kernel), [(size_py, tiles, cells_y, LANES)], values, y_table
     )
-    values = spread(values, "py")
+    values = spread_call(values, "py", 3)
     shapes = []
     heights = []
     size = (cells_x, cells_y, length_z)
@@ -423,13 +469,13 @@
         z_back,
         scratch=[held],
     )
-    coarse = spread(coarse, "py")
+    coarse = spread_call(coarse, "py", 4)
 
     def pick(*refs):
         pick_kernel(heights, *refs)
 
     (coarse,) = call(pick, [coarse.shape], group_table, coarse, scalars=1)
-    coarse = spread(coarse, "py")
+    coarse = spread_call(coarse, "py", 5)
     routed, start = [], 0
     for shape, height in zip(shapes, heights):
         routed.append(coarse[:, start : start + height, : shape[3]].reshape(shape))

time: 154 us -> 160 us (1.039)
  Pallas kernels: 16.6 us -> 139 us
  blocking collectives: 108 us -> 0 us
  waiting for transfers between devices: 19.2 us -> 0 us
  local copies, waits for them, and re-layouts: 5.12 us -> 19.2 us
  starting transfers between devices: 3.85 us -> 0 us
    pallas_call x0 -> x6, Pallas kernels: none -> 124 us  [spread_call(): pl.pallas_call(body, out_shape=jax.ShapeDtypeStruct(values.shape, values....]
    all_to_all x5 -> x0, blocking collectives: 108 us -> none  [spread(): return lax.all_to_all(values, axis, split_axis=0, concat_axis=0, tiled=True)]
    all_to_all x1 -> x0, waiting for transfers between devices: 19.2 us -> none  [spread(): return lax.all_to_all(values, axis, split_axis=0, concat_axis=0, tiled=True)]
    unnamed x16 -> x38, local copies, waits for them, and re-layouts: 3.24 us -> 14.9 us
    all_to_all x1 -> x0, starting transfers between devices: 3.85 us -> none  [spread(): return lax.all_to_all(values, axis, split_axis=0, concat_axis=0, tiled=True)]
    slice x3, local copies, waits for them, and re-layouts: 1.88 us -> 4.3 us  [lanes_path(): routed.append(coarse[:, start:start + height, :shape[3]].reshape(shape))]
  transfers between devices with their start and end apart: 1 -> 0, of which waited for: 1 -> 0; matrix products, arithmetic and copies ran while one was open for 0% -> 0% of each run, Pallas kernels for 0% -> 0%
where the time goes in v3:
time: 160 us; the launch traced here: 159 us
  Pallas kernels  139 us (87%)
  local copies, waits for them, and re-layouts  19.2 us (12%)
    pallas_call x6, Pallas kernels, spread_call(): pl.pallas_call(body, out_shape=jax.ShapeDtypeStruct(values.shape, values....  124 us
    pallas_call x6, Pallas kernels, call(): pl.pallas_call(body, out_shape=out, in_specs=specs, out_specs=[pl.BlockSp...  15.4 us
    unnamed x38, local copies, waits for them, and re-layouts  14.9 us
    slice x3, local copies, waits for them, and re-layouts, lanes_path(): routed.append(coarse[:, start:start + height, :shape[3]].reshape(shape))  4.3 us

profile of v3, /device:TPU:0, one launch (start us, length us, event | category | flops | bytes accessed | tf_op | source)
XLA Modules:
  0.0 159.2 jit_solution(1769477618769279660)
XLA Ops:
  0.6 0.0 copy-start.9
  0.7 1.2 copy-done.9
  1.9 0.0 copy-start.12
  1.9 1.0 copy-done.12
  2.9 0.0 copy-start.14
  2.9 0.9 copy-done.14
  3.9 1.8 %shard_map.111.refs_0_ = f32[8,11,32,128]{3,2,1,0:T(8,128)S(1)} custom-call(f32[2,16,32,256]{3,2,1,0:T(8,128)S(1)} %copy-done.9, f32[16,32,256]{2,1,0:T(8,128)S(1)} %copy-done.12, f32[256,256]{1,0:T(8,128)S(1)} %copy-done.14), custom_call_target="tpu_custom_call" | custom-call | tf_op jit(solution)/shard_map/pallas_call | solution.py:397
  5.6 0.0 copy-start.3
  5.7 1.1 copy-done.3
  6.8 0.0 copy-start.8
  6.8 31.5 %shard_map.112.refs_0_ = f32[8,11,32,128]{3,2,1,0:T(8,128)} custom-call(f32[8,11,32,128]{3,2,1,0:T(8,128)} %copy-done.3), custom_call_target="tpu_custom_call" | custom-call | tf_op jit(solution)/shard_map/pallas_call | solution.py:369
  38.3 0.0 copy-done.8
  38.3 0.0 copy-start.2
  38.3 1.4 copy-done.2
  39.6 2.2 %shard_map.113.refs_0_ = f32[4,768,128]{2,1,0:T(8,128)S(1)} custom-call(f32[8,11,32,128]{3,2,1,0:T(8,128)S(1)} %copy-done.2, f32[512,256]{1,0:T(8,128)S(1)} %copy-done.8), custom_call_target="tpu_custom_call" | custom-call | tf_op jit(solution)/shard_map/pallas_call | solution.py:397
  41.8 0.0 copy-start.1
  41.8 1.2 copy-done.1
  43.0 23.9 %shard_map.114.refs_1_ = f32[4,768,128]{2,1,0:T(8,128)} custom-call(f32[4,768,128]{2,1,0:T(8,128)} %copy-done.1), custom_call_target="tpu_custom_call" | custom-call | tf_op jit(solution)/shard_map/pallas_call | solution.py:369
  66.9 0.0 copy-done.16
  66.9 0.0 copy-done.17
  66.9 0.0 copy-start
  66.9 1.4 copy-done
  68.3 2.8 %shard_map.115.refs_0_ = f32[4,512,128]{2,1,0:T(8,128)S(1)} custom-call(s32[1]{0:T(128)} %bitcast.refs_0_, f32[4,768,128]{2,1,0:T(8,128)S(1)} %copy-done, f32[128,128]{1,0:T(8,128)S(1)} %copy-done.17, f32[128,128]{1,0:T(8,128)S(1)} %copy-done.16), custom_call_target="tpu_custom_call" | custom-call | tf_op jit(solution)/shard_map/pallas_call | solution.py:397
  71.1 0.0 copy-start.5
  71.1 1.0 copy-done.5
  72.1 17.1 %shard_map.116.refs_0_ = f32[4,512,128]{2,1,0:T(8,128)} custom-call(f32[4,512,128]{2,1,0:T(8,128)} %copy-done.5), custom_call_target="tpu_custom_call" | custom-call | tf_op jit(solution)/shard_map/pallas_call | solution.py:369
  89.2 0.0 copy-start.6
  89.2 1.2 copy-done.6
  90.5 2.1 %shard_map.117.refs_0_ = f32[8,8,32,128]{3,2,1,0:T(8,128)S(1)} custom-call(f32[4,512,128]{2,1,0:T(8,128)S(1)} %copy-done.6, f32[512,256]{1,0:T(8,128)S(1)} %copy-done.8), custom_call_target="tpu_custom_call" | custom-call | tf_op jit(solution)/shard_map/pallas_call | solution.py:397
  92.6 0.0 copy-start.7
  92.6 1.0 copy-done.7
  93.6 28.0 %shard_map.118.refs_0_ = f32[8,8,32,128]{3,2,1,0:T(8,128)} custom-call(f32[8,8,32,128]{3,2,1,0:T(8,128)} %copy-done.7), custom_call_target="tpu_custom_call" | custom-call | tf_op jit(solution)/shard_map/pallas_call | solution.py:369
  121.6 0.0 copy-done.13
  121.6 0.0 copy-start.4
  121.6 1.2 copy-done.4
  122.9 5.9 %shard_map.119 = (f32[2,16,32,256]{3,2,1,0:T(8,128)}, f32[8,42,128]{2,1,0:T(8,128)S(1)}) custom-call(f32[8,8,32,128]{3,2,1,0:T(8,128)S(1)} %copy-done.4, f32[256,256]{1,0:T(8,128)S(1)} %copy-done.13), custom_call_target="tpu_custom_call" | custom-call | tf_op jit(solution)/shard_map/pallas_call | solution.py:397
  128.8 0.7 copy-done.15
  129.5 14.1 %shard_map.120.refs_1_ = f32[8,42,128]{2,1,0:T(8,128)} custom-call(f32[8,42,128]{2,1,0:T(8,128)} %copy-done.15), custom_call_target="tpu_custom_call" | custom-call | tf_op jit(solution)/shard_map/pallas_call | solution.py:369
  143.6 0.0 copy-done.18
  143.6 0.0 copy-start.10
  143.6 0.9 copy-done.10
  144.5 0.6 shard_map.121.refs_0_
  145.1 0.0 copy-start.11
  145.1 0.7 copy-done.11
  145.8 9.1 %shard_map.122 = f32[8,42,128]{2,1,0:T(8,128)} custom-call(f32[8,42,128]{2,1,0:T(8,128)} %copy-done.11), custom_call_target="tpu_custom_call" | custom-call | tf_op jit(solution)/shard_map/pallas_call | solution.py:369
  154.9 1.4 slice.11
  156.3 1.4 slice.10
  157.6 1.6 slice.9
  (5 shorter events, 0.0 us)
Async XLA Ops:
  0.6 1.2 copy-start.9
  1.9 1.0 copy-start.12
  2.9 0.9 copy-start.14
  5.6 1.1 copy-start.3
  6.8 31.5 %copy-start.8 = (f32[512,256]{1,0:T(8,128)S(1)}, f32[512,256]{1,0:T(8,128)}, u32[]{:S(2)}) copy-start(f32[512,256]{1,0:T(8,128)} %constant.24.clone.refs_1_) | copy-start | bytes 1572868
  38.3 1.4 copy-start.2
  41.8 1.2 copy-start.1
  43.0 23.9 %copy-start.16 = (f32[128,128]{1,0:T(8,128)S(1)}, f32[128,128]{1,0:T(8,128)}, u32[]{:S(2)}) copy-start(f32[128,128]{1,0:T(8,128)} %constant.26.clone.refs_3_) | copy-start | bytes 196612
  43.0 23.9 %copy-start.17 = (f32[128,128]{1,0:T(8,128)S(1)}, f32[128,128]{1,0:T(8,128)}, u32[]{:S(2)}) copy-start(f32[128,128]{1,0:T(8,128)} %constant.25.clone.refs_2_) | copy-start | bytes 196612
  66.9 1.4 copy-start
  71.1 1.0 copy-start.5
  89.2 1.2 copy-start.6
  92.6 1.0 copy-start.7
  93.6 28.1 %copy-start.13 = (f32[256,256]{1,0:T(8,128)S(1)}, f32[256,256]{1,0:T(8,128)}, u32[]{:S(2)}) copy-start(f32[256,256]{1,0:T(8,128)} %constant.30.refs_1_) | copy-start | bytes 786436
  93.6 50.0 %copy-start.18 = (s32[3,8]{1,0:T(4,128)S(1)}, s32[3,8]{1,0:T(4,128)}, u32[]{:S(2)}) copy-start(s32[3,8]{1,0:T(4,128)} %refs_0_.3) | copy-start | bytes 292
  121.6 1.2 copy-start.4
  128.8 0.7 copy-start.15
  143.6 0.9 copy-start.10
  145.1 0.7 copy-start.11

commit v4 on v3

--- a/solution.py
+++ b/solution.py
@@ -332,9 +332,11 @@
             start += height
 
 
-def spread_kernel(axis, in_ref, out_ref, own_sem, send_sems, recv_sems):
-    count = in_ref.shape[0]
+def spread_kernel(axis, tail, used, in_ref, out_ref, own_sem, sends, recvs, tail_sends, tail_recvs):
+    count, height = in_ref.shape[0], in_ref.shape[1]
     me = lax.axis_index(axis)
+    used = used()
+    rest = pl.ds(tail, height - tail)
     barrier = pltpu.get_barrier_semaphore()
     for away in range(1, count):
         peer = lax.rem(me + away, count)
@@ -342,42 +344,62 @@
     own = pltpu.make_async_copy(in_ref.at[me], out_ref.at[me], own_sem)
     own.start()
     pl.semaphore_wait(barrier, count - 1)
-    copies = []
+    copies, extras = [], []
     for away in range(1, count):
         peer = lax.rem(me + away, count)
         copy = pltpu.make_async_remote_copy(
-            src_ref=in_ref.at[peer],
-            dst_ref=out_ref.at[me],
-            send_sem=send_sems.at[away],
-            recv_sem=recv_sems.at[away],
+            src_ref=in_ref.at[peer, pl.ds(0, tail)],
+            dst_ref=out_ref.at[me, pl.ds(0, tail)],
+            send_sem=sends.at[away],
+            recv_sem=recvs.at[away],
             device_id={axis: peer},
             device_id_type=MESH,
         )
         copy.start()
         copies.append(copy)
+    for source in range(1, count):
+        extra = pltpu.make_async_remote_copy(
+            src_ref=in_ref.at[0, rest],
+            dst_ref=out_ref.at[source, rest],
+            send_sem=tail_sends.at[source],
+            recv_sem=tail_recvs.at[source],
+            device_id={axis: 0},
+            device_id_type=MESH,
+        )
+        pl.when((me == source) & used)(extra.start)
+        extras.append(extra)
+    for source in range(count):
+
+        @pl.when((me != source) & jnp.logical_not((me == 0) & used))
+        def _():
+            out_ref[source, rest] = jnp.zeros(out_ref.shape[1:], jnp.float32)[tail:]
+
     own.wait()
     for copy in copies:
         copy.wait()
-
-
-def spread_call(values, axis, number):
+    for source in range(1, count):
+        pl.when((me == source) & used)(extras[source - 1].wait_send)
+        pl.when((me == 0) & used)(extras[source - 1].wait_recv)
+
+
+def spread_call(values, axis, number, tail, used):
     count = values.shape[0]
 
     def body(*refs):
-        spread_kernel(axis, *refs)
+        spread_kernel(axis, tail, used, *refs)
 
     return pl.pallas_call(
         body,
         out_shape=jax.ShapeDtypeStruct(values.shape, values.dtype),
         in_specs=[pl.BlockSpec(memory_space=pltpu.VMEM)],
         out_specs=pl.BlockSpec(memory_space=pltpu.VMEM),
-        scratch_shapes=[
-            pltpu.SemaphoreType.DMA,
-            pltpu.SemaphoreType.DMA((count,)),
-            pltpu.SemaphoreType.DMA((count,)),
-        ],
+        scratch_shapes=[pltpu.SemaphoreType.DMA] + [pltpu.SemaphoreType.DMA((count,))] * 4,
         compiler_params=pltpu.CompilerParams(collective_id=number, has_side_effects=True),
     )(values)
+
+
+def spread(values, axis):
+    return lax.all_to_all(values, axis, split_axis=0, concat_axis=0, tiled=True)
 
 
 def lanes_path(white_noise, spectrum, group_table):
@@ -436,11 +458,13 @@
         z_ahead,
         scratch=[held],
     )
-    values = spread_call(values, "py", 0)
+    values = spread_call(values, "py", 0, tiles + hi, lambda: True)
     (values,) = call(
         bind(y_forward_kernel), [(size_px, 3 * length_y, LANES)], values, y_table
     )
-    values = spread_call(values, "px", 1)
+    values = spread_call(
+        values, "px", 1, 2 * length_y + length_y // 2, lambda: lax.axis_index("py") == 0
+    )
     (values,) = call(
         bind(x_kernel),
         [(size_px, 2 * length_y, LANES)],
@@ -450,11 +474,11 @@
         x_table(1.0),
         scalars=1,
     )
-    values = spread_call(values, "px", 2)
+    values = spread(values, "px")
     (values,) = call(
         bind(y_back_kernel), [(size_py, tiles, cells_y, LANES)], values, y_table
     )
-    values = spread_call(values, "py", 3)
+    values = spread(values, "py")
     shapes = []
     heights = []
     size = (cells_x, cells_y, length_z)
@@ -469,13 +493,13 @@
         z_back,
         scratch=[held],
     )
-    coarse = spread_call(coarse, "py", 4)
+    coarse = spread(coarse, "py")
 
     def pick(*refs):
         pick_kernel(heights, *refs)
 
     (coarse,) = call(pick, [coarse.shape], group_table, coarse, scalars=1)
-    coarse = spread_call(coarse, "py", 5)
+    coarse = spread(coarse, "py")
     routed, start = [], 0
     for shape, height in zip(shapes, heights):
         routed.append(coarse[:, start : start + height, : shape[3]].reshape(shape))

time: 160 us -> 152 us (0.950)
  blocking collectives: 0 us -> 71.3 us
  Pallas kernels: 139 us -> 69.3 us
  local copies, waits for them, and re-layouts: 19.2 us -> 10.1 us
    all_to_all x0 -> x4, blocking collectives: none -> 71.3 us  [spread(): return lax.all_to_all(values, axis, split_axis=0, concat_axis=0, tiled=True)]
    pallas_call x6 -> x2, Pallas kernels: 124 us -> 53.9 us  [spread_call(): pl.pallas_call(body, out_shape=jax.ShapeDtypeStruct(values.shape, values....]
    unnamed x38 -> x24, local copies, waits for them, and re-layouts: 14.9 us -> 8.27 us
    slice x3, local copies, waits for them, and re-layouts: 4.3 us -> 1.88 us  [lanes_path(): routed.append(coarse[:, start:start + height, :shape[3]].reshape(shape))]
where the time goes in v4:
time: 152 us
  blocking collectives  71.3 us (47%)
  Pallas kernels  69.3 us (46%)
  local copies, waits for them, and re-layouts  10.1 us (7%)
    all_to_all x4, blocking collectives, spread(): return lax.all_to_all(values, axis, split_axis=0, concat_axis=0, tiled=True)  71.3 us
    pallas_call x2, Pallas kernels, spread_call(): pl.pallas_call(body, out_shape=jax.ShapeDtypeStruct(values.shape, values....  53.9 us
    pallas_call x6, Pallas kernels, call(): pl.pallas_call(body, out_shape=out, in_specs=specs, out_specs=[pl.BlockSp...  15.4 us
    unnamed x24, local copies, waits for them, and re-layouts  8.27 us

profile of v4, /device:TPU:0, one launch (start us, length us, event | category | flops | bytes accessed | tf_op | source)
XLA Modules:
  0.0 151.5 jit_solution(15421619341974383422)
XLA Ops:
  0.6 0.0 copy-start.5
  0.7 1.2 copy-done.5
  1.9 0.0 copy-start.6
  1.9 1.0 copy-done.6
  2.9 0.0 copy-start.8
  2.9 0.9 copy-done.8
  3.9 1.8 %shard_map.111.refs_0_ = f32[8,11,32,128]{3,2,1,0:T(8,128)S(1)} custom-call(f32[2,16,32,256]{3,2,1,0:T(8,128)S(1)} %copy-done.5, f32[16,32,256]{2,1,0:T(8,128)S(1)} %copy-done.6, f32[256,256]{1,0:T(8,128)S(1)} %copy-done.8), custom_call_target="tpu_custom_call" | custom-call | tf_op jit(solution)/shard_map/pallas_call | solution.py:419
  5.7 0.0 copy-start.3
  5.7 1.1 copy-done.3
  6.8 0.0 copy-start.4
  6.8 38.2 %shard_map.112.refs_0_ = f32[8,11,32,128]{3,2,1,0:T(8,128)} custom-call(f32[8,11,32,128]{3,2,1,0:T(8,128)} %copy-done.3), custom_call_target="tpu_custom_call" | custom-call | tf_op jit(solution)/shard_map/pallas_call | solution.py:391
  45.0 0.0 copy-done.4
  45.0 0.0 copy-start.2
  45.0 1.4 copy-done.2
  46.3 2.2 %shard_map.113.refs_0_ = f32[4,768,128]{2,1,0:T(8,128)S(1)} custom-call(f32[8,11,32,128]{3,2,1,0:T(8,128)S(1)} %copy-done.2, f32[512,256]{1,0:T(8,128)S(1)} %copy-done.4), custom_call_target="tpu_custom_call" | custom-call | tf_op jit(solution)/shard_map/pallas_call | solution.py:419
  48.5 0.0 copy-start.1
  48.5 1.2 copy-done.1
  49.7 0.0 copy-start.9
  49.7 0.0 copy-start.10
  49.7 15.7 %shard_map.114.refs_1_ = f32[4,768,128]{2,1,0:T(8,128)} custom-call(f32[4,768,128]{2,1,0:T(8,128)} %copy-done.1), custom_call_target="tpu_custom_call" | custom-call | tf_op jit(solution)/shard_map/pallas_call | solution.py:391
  65.4 0.0 copy-done.9
  65.4 0.0 copy-done.10
  65.4 0.0 copy-start
  65.4 1.4 copy-done
  66.8 2.8 %shard_map.115 = f32[4,512,128]{2,1,0:T(8,128)S(1)} custom-call(s32[1]{0:T(128)} %bitcast.refs_0_, f32[4,768,128]{2,1,0:T(8,128)S(1)} %copy-done, f32[128,128]{1,0:T(8,128)S(1)} %copy-done.10, f32[128,128]{1,0:T(8,128)S(1)} %copy-done.9), custom_call_target="tpu_custom_call" | custom-call | tf_op jit(solution)/shard_map/pallas_call | solution.py:419
  69.6 12.4 %all_to_all.20.refs_0_ = f32[4,512,128]{2,1,0:T(8,128)S(1)} all-to-all(f32[4,512,128]{2,1,0:T(8,128)S(1)} %shard_map.115), channel_id=1, replica_groups=mesh['px'=4,'py'=8] {'px'}, dimensions={0} | all-to-all | bytes 2097152 | tf_op jit(solution)/shard_map/all_to_all | solution.py:402
  82.0 2.2 %shard_map.116 = f32[8,8,32,128]{3,2,1,0:T(8,128)S(1)} custom-call(f32[4,512,128]{2,1,0:T(8,128)S(1)} %all_to_all.20.refs_0_, f32[512,256]{1,0:T(8,128)S(1)} %copy-done.4), custom_call_target="tpu_custom_call" | custom-call | tf_op jit(solution)/shard_map/pallas_call | solution.py:419
  84.1 0.0 copy-start.7
  84.1 0.0 copy-start.11
  84.2 37.5 %all_to_all.21.refs_0_ = f32[8,8,32,128]{3,2,1,0:T(8,128)S(1)} all-to-all(f32[8,8,32,128]{3,2,1,0:T(8,128)S(1)} %shard_map.116), channel_id=1, replica_groups=mesh['px'=4,'py'=8] {'py'}, dimensions={0} | all-to-all | bytes 2097152 | tf_op jit(solution)/shard_map/all_to_all | solution.py:402
  121.7 0.0 copy-done.7
  121.7 5.9 %shard_map.117 = (f32[2,16,32,256]{3,2,1,0:T(8,128)}, f32[8,42,128]{2,1,0:T(8,128)S(1)}) custom-call(f32[8,8,32,128]{3,2,1,0:T(8,128)S(1)} %all_to_all.21.refs_0_, f32[256,256]{1,0:T(8,128)S(1)} %copy-done.7), custom_call_target="tpu_custom_call" | custom-call | tf_op jit(solution)/shard_map/pallas_call | solution.py:419
  127.6 10.7 %all_to_all.22.refs_1_ = f32[8,42,128]{2,1,0:T(8,128)S(1)} all-to-all(f32[8,42,128]{2,1,0:T(8,128)S(1)} %get-tuple-element.7), channel_id=1, replica_groups=mesh['px'=4,'py'=8] {'py'}, dimensions={0} | all-to-all | bytes 344064 | tf_op jit(solution)/shard_map/all_to_all | solution.py:402
  138.3 0.0 copy-done.11
  138.3 0.6 shard_map.118
  138.9 10.7 %all_to_all.23 = f32[8,42,128]{2,1,0:T(8,128)S(1)} all-to-all(f32[8,42,128]{2,1,0:T(8,128)S(1)} %shard_map.118), channel_id=1, replica_groups=mesh['px'=4,'py'=8] {'py'}, dimensions={0} | all-to-all | bytes 344064 | tf_op jit(solution)/shard_map/all_to_all | solution.py:402
  149.6 0.6 slice.14
  150.2 0.6 slice.13
  150.9 0.7 slice.12
Async XLA Ops:
  0.6 1.2 copy-start.5
  1.9 1.0 copy-start.6
  2.9 0.9 copy-start.8
  5.7 1.1 copy-start.3
  6.8 38.2 %copy-start.4 = (f32[512,256]{1,0:T(8,128)S(1)}, f32[512,256]{1,0:T(8,128)}, u32[]{:S(2)}) copy-start(f32[512,256]{1,0:T(8,128)} %constant.24.clone.refs_1_) | copy-start | bytes 1572868
  45.0 1.4 copy-start.2
  48.5 1.2 copy-start.1
  49.7 15.7 %copy-start.9 = (f32[128,128]{1,0:T(8,128)S(1)}, f32[128,128]{1,0:T(8,128)}, u32[]{:S(2)}) copy-start(f32[128,128]{1,0:T(8,128)} %constant.26.clone.refs_3_) | copy-start | bytes 196612
  49.7 15.7 %copy-start.10 = (f32[128,128]{1,0:T(8,128)S(1)}, f32[128,128]{1,0:T(8,128)}, u32[]{:S(2)}) copy-start(f32[128,128]{1,0:T(8,128)} %constant.25.clone.refs_2_) | copy-start | bytes 196612
  65.4 1.4 copy-start
  84.1 37.6 %copy-start.7 = (f32[256,256]{1,0:T(8,128)S(1)}, f32[256,256]{1,0:T(8,128)}, u32[]{:S(2)}) copy-start(f32[256,256]{1,0:T(8,128)} %constant.30.refs_1_) | copy-start | bytes 786436
  84.1 54.2 %copy-start.11 = (s32[3,8]{1,0:T(4,128)S(1)}, s32[3,8]{1,0:T(4,128)}, u32[]{:S(2)}) copy-start(s32[3,8]{1,0:T(4,128)} %refs_0_.3) | copy-start | bytes 292

commit v5 on v4

--- a/solution.py
+++ b/solution.py
@@ -345,7 +345,7 @@
     own.start()
     pl.semaphore_wait(barrier, count - 1)
     copies, extras = [], []
-    for away in range(1, count):
+    for away in sorted(range(1, count), key=lambda a: -min(a, count - a)):
         peer = lax.rem(me + away, count)
         copy = pltpu.make_async_remote_copy(
             src_ref=in_ref.at[peer, pl.ds(0, tail)],

time: 152 us -> 152 us (level)
  no operation moved by 1% of the time
where the time goes in v5:
time: 152 us
  blocking collectives  71.5 us (47%)
  Pallas kernels  69.2 us (46%)
  local copies, waits for them, and re-layouts  10.1 us (7%)
    all_to_all x4, blocking collectives, spread(): return lax.all_to_all(values, axis, split_axis=0, concat_axis=0, tiled=True)  71.5 us
    pallas_call x2, Pallas kernels, spread_call(): pl.pallas_call(body, out_shape=jax.ShapeDtypeStruct(values.shape, values....  53.8 us
    pallas_call x6, Pallas kernels, call(): pl.pallas_call(body, out_shape=out, in_specs=specs, out_specs=[pl.BlockSp...  15.4 us
    unnamed x24, local copies, waits for them, and re-layouts  8.27 us

profile of v5, /device:TPU:0, one launch (start us, length us, event | category | flops | bytes accessed | tf_op | source)
XLA Modules:
  0.0 151.7 jit_solution(1385327475593737504)
XLA Ops:
  0.6 0.0 copy-start.5
  0.7 1.2 copy-done.5
  1.9 0.0 copy-start.6
  1.9 1.0 copy-done.6
  2.9 0.0 copy-start.8
  2.9 0.9 copy-done.8
  3.9 1.8 %shard_map.111.refs_0_ = f32[8,11,32,128]{3,2,1,0:T(8,128)S(1)} custom-call(f32[2,16,32,256]{3,2,1,0:T(8,128)S(1)} %copy-done.5, f32[16,32,256]{2,1,0:T(8,128)S(1)} %copy-done.6, f32[256,256]{1,0:T(8,128)S(1)} %copy-done.8), custom_call_target="tpu_custom_call" | custom-call | tf_op jit(solution)/shard_map/pallas_call | solution.py:419
  5.7 0.0 copy-start.3
  5.7 1.1 copy-done.3
  6.8 0.0 copy-start.4
  6.8 38.1 %shard_map.112.refs_0_ = f32[8,11,32,128]{3,2,1,0:T(8,128)} custom-call(f32[8,11,32,128]{3,2,1,0:T(8,128)} %copy-done.3), custom_call_target="tpu_custom_call" | custom-call | tf_op jit(solution)/shard_map/pallas_call | solution.py:391
  44.9 0.0 copy-done.4
  44.9 0.0 copy-start.2
  44.9 1.4 copy-done.2
  46.3 2.2 %shard_map.113.refs_0_ = f32[4,768,128]{2,1,0:T(8,128)S(1)} custom-call(f32[8,11,32,128]{3,2,1,0:T(8,128)S(1)} %copy-done.2, f32[512,256]{1,0:T(8,128)S(1)} %copy-done.4), custom_call_target="tpu_custom_call" | custom-call | tf_op jit(solution)/shard_map/pallas_call | solution.py:419
  48.5 0.0 copy-start.1
  48.5 1.2 copy-done.1
  49.6 0.0 copy-start.9
  49.6 0.0 copy-start.10
  49.6 15.7 %shard_map.114.refs_1_ = f32[4,768,128]{2,1,0:T(8,128)} custom-call(f32[4,768,128]{2,1,0:T(8,128)} %copy-done.1), custom_call_target="tpu_custom_call" | custom-call | tf_op jit(solution)/shard_map/pallas_call | solution.py:391
  65.3 0.0 copy-done.9
  65.3 0.0 copy-done.10
  65.4 0.0 copy-start
  65.4 1.4 copy-done
  66.8 2.8 %shard_map.115 = f32[4,512,128]{2,1,0:T(8,128)S(1)} custom-call(s32[1]{0:T(128)} %bitcast.refs_0_, f32[4,768,128]{2,1,0:T(8,128)S(1)} %copy-done, f32[128,128]{1,0:T(8,128)S(1)} %copy-done.10, f32[128,128]{1,0:T(8,128)S(1)} %copy-done.9), custom_call_target="tpu_custom_call" | custom-call | tf_op jit(solution)/shard_map/pallas_call | solution.py:419
  69.6 12.4 %all_to_all.20.refs_0_ = f32[4,512,128]{2,1,0:T(8,128)S(1)} all-to-all(f32[4,512,128]{2,1,0:T(8,128)S(1)} %shard_map.115), channel_id=1, replica_groups=mesh['px'=4,'py'=8] {'px'}, dimensions={0} | all-to-all | bytes 2097152 | tf_op jit(solution)/shard_map/all_to_all | solution.py:402
  81.9 2.1 %shard_map.116 = f32[8,8,32,128]{3,2,1,0:T(8,128)S(1)} custom-call(f32[4,512,128]{2,1,0:T(8,128)S(1)} %all_to_all.20.refs_0_, f32[512,256]{1,0:T(8,128)S(1)} %copy-done.4), custom_call_target="tpu_custom_call" | custom-call | tf_op jit(solution)/shard_map/pallas_call | solution.py:419
  84.1 0.0 copy-start.7
  84.1 0.0 copy-start.11
  84.1 37.7 %all_to_all.21.refs_0_ = f32[8,8,32,128]{3,2,1,0:T(8,128)S(1)} all-to-all(f32[8,8,32,128]{3,2,1,0:T(8,128)S(1)} %shard_map.116), channel_id=1, replica_groups=mesh['px'=4,'py'=8] {'py'}, dimensions={0} | all-to-all | bytes 2097152 | tf_op jit(solution)/shard_map/all_to_all | solution.py:402
  121.8 0.0 copy-done.7
  121.8 5.9 %shard_map.117 = (f32[2,16,32,256]{3,2,1,0:T(8,128)}, f32[8,42,128]{2,1,0:T(8,128)S(1)}) custom-call(f32[8,8,32,128]{3,2,1,0:T(8,128)S(1)} %all_to_all.21.refs_0_, f32[256,256]{1,0:T(8,128)S(1)} %copy-done.7), custom_call_target="tpu_custom_call" | custom-call | tf_op jit(solution)/shard_map/pallas_call | solution.py:419
  127.8 10.7 %all_to_all.22.refs_1_ = f32[8,42,128]{2,1,0:T(8,128)S(1)} all-to-all(f32[8,42,128]{2,1,0:T(8,128)S(1)} %get-tuple-element.7), channel_id=1, replica_groups=mesh['px'=4,'py'=8] {'py'}, dimensions={0} | all-to-all | bytes 344064 | tf_op jit(solution)/shard_map/all_to_all | solution.py:402
  138.5 0.0 copy-done.11
  138.5 0.6 shard_map.118
  139.1 10.7 %all_to_all.23 = f32[8,42,128]{2,1,0:T(8,128)S(1)} all-to-all(f32[8,42,128]{2,1,0:T(8,128)S(1)} %shard_map.118), channel_id=1, replica_groups=mesh['px'=4,'py'=8] {'py'}, dimensions={0} | all-to-all | bytes 344064 | tf_op jit(solution)/shard_map/all_to_all | solution.py:402
  149.8 0.6 slice.14
  150.4 0.6 slice.13
  151.0 0.7 slice.12
Async XLA Ops:
  0.6 1.2 copy-start.5
  1.9 1.0 copy-start.6
  2.9 0.9 copy-start.8
  5.7 1.1 copy-start.3
  6.8 38.2 %copy-start.4 = (f32[512,256]{1,0:T(8,128)S(1)}, f32[512,256]{1,0:T(8,128)}, u32[]{:S(2)}) copy-start(f32[512,256]{1,0:T(8,128)} %constant.24.clone.refs_1_) | copy-start | bytes 1572868
  44.9 1.4 copy-start.2
  48.5 1.2 copy-start.1
  49.6 15.7 %copy-start.9 = (f32[128,128]{1,0:T(8,128)S(1)}, f32[128,128]{1,0:T(8,128)}, u32[]{:S(2)}) copy-start(f32[128,128]{1,0:T(8,128)} %constant.26.clone.refs_3_) | copy-start | bytes 196612
  49.6 15.7 %copy-start.10 = (f32[128,128]{1,0:T(8,128)S(1)}, f32[128,128]{1,0:T(8,128)}, u32[]{:S(2)}) copy-start(f32[128,128]{1,0:T(8,128)} %constant.25.clone.refs_2_) | copy-start | bytes 196612
  65.4 1.4 copy-start
  84.1 37.8 %copy-start.7 = (f32[256,256]{1,0:T(8,128)S(1)}, f32[256,256]{1,0:T(8,128)}, u32[]{:S(2)}) copy-start(f32[256,256]{1,0:T(8,128)} %constant.30.refs_1_) | copy-start | bytes 786436
  84.1 54.4 %copy-start.11 = (s32[3,8]{1,0:T(4,128)S(1)}, s32[3,8]{1,0:T(4,128)}, u32[]{:S(2)}) copy-start(s32[3,8]{1,0:T(4,128)} %refs_0_.3) | copy-start | bytes 292
